TPU v7x, 32 devices: a whole 2x2x4 slice. The times are simulated.
32 devices in a mesh: ens: 4 (over y, x), lon: 8 (over z, core).
Axes of the slice: x: 2, y: 2, z: 4, core: 2. Of those that a mesh axis runs over, the one named last changes fastest.
Arguments:
- control: float32 [8, 1024, 512], P('ens', None, 'lon'), may hold values from -6 to 6
- residual: float32 [8, 1024, 512], P('ens', None, 'lon'), may hold values from -6 to 6
- direction: float32 [8, 1024, 512], P('ens', None, 'lon'), may hold values from -6 to 6
- ens_perturb: bfloat16 [8, 3, 1024, 512], P('ens', None, None, 'lon'), may hold values from -1.5 to 1.5
- localize: float32 [1024, 1024], replicated, may hold values from -0.5 to 1.5
- obs_cell: int32 [32768], P('lon'), may hold values from 0 to 65535
- obs_slot: int32 [32768], P('lon'), may hold values from 0 to 3
- obs_weight: float32 [32768], P('lon'), may hold values from 0.5 to 4
Outputs:
- control_new: float32 [8, 1024, 512], P('ens', None, 'lon')
- residual_new: float32 [8, 1024, 512], P('ens', None, 'lon')
- direction_new: float32 [8, 1024, 512], P('ens', None, 'lon')
Inputs may be any that keep to these rules, and one draw needn't show every extreme that they name: `obs_cell`: row-major cell within the entry's own longitude tile: row times 64 plus column. `obs_slot`: slot n < 3 observes the height after model step n + 1; slot 3 marks a padding entry that observes nothing.
All inputs are finite; a program needn't handle non-finite values.
Results may differ from a plain program's by a relative error of at most 0.0003.
Values sent between devices are 32-bit elements; how exact they have to be, the bound alone decides.
A program may use at most 64 MiB of HBM per device.

v0:
```python
import functools
import itertools

import numpy as np
import jax
import jax.numpy as jnp
from jax import lax
from jax.experimental import pallas as pl
from jax.experimental.pallas import tpu as pltpu
from jax.sharding import PartitionSpec as P

STEPS = 3
HALO = 8
CHUNK = 512
MESH = pl.DeviceIdType.MESH
NT = (((1,), (1,)), ((), ()))
NN = (((1,), (0,)), ((), ()))


def split_bf16(values):
    high = values.astype(jnp.bfloat16)
    low = (values - high.astype(jnp.float32)).astype(jnp.bfloat16)
    return high, low


def dot(left, right, dims):
    return lax.dot_general(left, right, dims, preferred_element_type=jnp.float32)


def grid_constants(lat):
    phi = np.pi * (-1.0 / 3.0 + 2.0 / 3.0 * (np.arange(lat) + 0.5) / lat)
    half = 0.5 * 0.35
    up = np.full(lat, half)
    up[-1] = 0.0
    down = np.full(lat, half)
    down[0] = 0.0
    rows = np.stack([half / np.cos(phi), 0.2 * np.sin(phi), up, down])
    return np.ascontiguousarray(np.broadcast_to(rows[:, None], (4, 8, lat))).astype(np.float32)


def linear_step(source, target, sign, consts, blocks):
    rows, lat = source.shape[1], source.shape[2]
    lon_c, cor_c, up_c, down_c = (sign * consts[k] for k in range(4))
    for start in blocks:
        here = pl.ds(start, 8)

        def east(comp, block):
            if start + 8 == rows:
                return pltpu.roll(block, 7, 0)
            return source[comp, pl.ds(start + 1, 8), :]

        def west(comp, block):
            if start == 0:
                return pltpu.roll(block, 1, 0)
            return source[comp, pl.ds(start - 1, 8), :]

        def lat_diff(block):
            return up_c * pltpu.roll(block, lat - 1, 1) - down_c * pltpu.roll(block, 1, 1)

        height, zonal, merid = (source[c, here, :] for c in range(3))
        height_lon = east(0, height) - west(0, height)
        zonal_lon = east(1, zonal) - west(1, zonal)
        target[0, here, :] = height - lon_c * zonal_lon - lat_diff(merid)
        target[1, here, :] = zonal - lon_c * height_lon + cor_c * merid
        target[2, here, :] = merid - lat_diff(height) - cor_c * zonal


def factors(ens):
    first = 2 if ens % 2 == 0 else 1
    return first, ens // first


def copy_count(ens):
    na, nb = factors(ens)
    cross = (na - 1) * (nb - 1)
    return 3 * (4 * cross + 3 * (na - 1 + nb - 1)) + 8


def kernel(
    ens, lon, direction, residual_hbm, perturb_hbm, localize_hbm, cell, slot, weight, consts,
    image, step_row, ratio_row,
    localize, residual, perturb, high, low, split, stage, relay0, relay1, arr_a, arr_b,
    reduced, fields, other, heights, wsum, wmat, tiles, tile,
    load_sem, send_sem, recv_sem, tile_send, tile_recv,
):
    na, nb = factors(ens)
    me_e, me_l = lax.axis_index("ens"), lax.axis_index("lon")
    me_a, me_b = me_e // nb, lax.rem(me_e, nb)
    count = ens * lon
    me = me_e * lon + me_l
    members, cols, lat = direction.shape
    block = lat // ens
    half = cols // 2
    stacked = members * cols
    halves = (pl.ds(0, half), pl.ds(half, half))
    inner = (pl.ds(HALO, half), pl.ds(HALO + half, half))

    def ens_of(i, j):
        return lax.rem(me_a + i, na) * nb + lax.rem(me_b + j, nb)

    def lanes_of(index):
        return pl.ds(pl.multiple_of(index * block, block), block)

    order = [(i, j) for i in range(1, na) for j in range(1, nb)]
    order += [(0, j) for j in range(1, nb)] + [(i, 0) for i in range(1, na)] + [(0, 0)]

    loads = {}
    for k, (i, j) in enumerate(order):
        at = lanes_of(ens_of(i, j))
        loads[i, j] = pltpu.make_async_copy(localize_hbm.at[at, :], localize.at[at, :], load_sem.at[k])
    load_p = pltpu.make_async_copy(perturb_hbm, perturb, load_sem.at[ens])
    load_r = pltpu.make_async_copy(residual_hbm, residual, load_sem.at[ens + 1])
    loads[order[0]].start()
    load_p.start()
    for key in order[1:]:
        loads[key].start()
    load_r.start()

    barrier = pltpu.get_barrier_semaphore()

    def greet(offset, carry):
        peer = lax.rem(me + offset, count)
        pl.semaphore_signal(
            barrier, inc=1, device_id=(peer // lon, lax.rem(peer, lon)), device_id_type=MESH
        )
        return carry

    lax.fori_loop(1, count, greet, 0)

    ids = itertools.count()

    def remote(src, dst, device):
        k = next(ids)
        return pltpu.make_async_remote_copy(
            src_ref=src, dst_ref=dst, send_sem=send_sem.at[k], recv_sem=recv_sem.at[k],
            device_id=device, device_id_type=MESH,
        )

    d_high, d_low = split_bf16(direction[...].reshape(stacked, lat))
    split[pl.ds(0, stacked), :] = d_high
    split[pl.ds(stacked, stacked), :] = d_low

    def localized_block(i, j):
        index = ens_of(i, j)
        at = lanes_of(index)
        loads[i, j].wait()
        l_high, l_low = split_bf16(localize[at, :])
        high[at, :] = l_high
        low[at, :] = l_low
        both = dot(split[...], l_high, NT)
        local = both[:stacked] + both[stacked:] + dot(split[pl.ds(0, stacked), :], l_low, NT)
        if (i, j) == order[0]:
            load_p.wait()
        for c in range(3):
            total = None
            for m in range(members):
                term = perturb[m, c, :, at].astype(jnp.float32) * local[m * cols:(m + 1) * cols]
                total = term if total is None else total + term
            stage[i * nb + j, c] = total

    def a_peer(i):
        return (ens_of(i, 0), me_l)

    def b_peer(j):
        return (ens_of(0, j), me_l)

    def part(i, j, c, h):
        return stage.at[i * nb + j, c, halves[h]]

    sum0, sum1, direct, relayed0, relayed1 = {}, {}, {}, {}, {}
    for c in range(3):
        for i in range(1, na):
            for j in range(1, nb):
                sum0[i, j, c] = remote(part(i, j, c, 0), relay0.at[j - 1, i - 1, c], b_peer(j))
                sum1[i, j, c] = remote(part(i, j, c, 1), relay1.at[i - 1, j - 1, c], a_peer(i))
        for j in range(1, nb):
            direct[0, j, c] = remote(part(0, j, c, 0), arr_b.at[j - 1, c, halves[0]], b_peer(j))
            relayed1[j, c] = remote(part(0, j, c, 1), arr_b.at[j - 1, c, halves[1]], b_peer(j))
        for i in range(1, na):
            direct[i, 0, c] = remote(part(i, 0, c, 1), arr_a.at[i - 1, c, halves[1]], a_peer(i))
            relayed0[i, c] = remote(part(i, 0, c, 0), arr_a.at[i - 1, c, halves[0]], a_peer(i))

    for k, (i, j) in enumerate(order):
        localized_block(i, j)
        if k == 0:
            pl.semaphore_wait(barrier, count - 1)
        for c in range(3):
            if i and j:
                sum0[i, j, c].start()
                sum1[i, j, c].start()
            elif i or j:
                direct[i, j, c].start()

    wsum[...] = jnp.zeros_like(wsum)
    slots_cols = STEPS * cols

    def weights(step, carry):
        at = pl.ds(pl.multiple_of(step * CHUNK, CHUNK), CHUNK)
        cells, slots, value = cell[:, at], slot[:, at], weight[:, at]
        row = cells // cols
        key = slots * cols + (cells - row * cols)
        v_high, v_low = split_bf16(value)
        v_high, v_low = v_high.astype(jnp.float32), v_low.astype(jnp.float32)
        ids = lax.broadcasted_iota(jnp.int32, (slots_cols, CHUNK), 0)
        hit = ids == key
        left = jnp.concatenate(
            [jnp.where(hit, v_high, 0.0), jnp.where(hit, v_low, 0.0)], axis=0
        ).astype(jnp.bfloat16)
        lat_ids = lax.broadcasted_iota(jnp.int32, (lat, CHUNK), 0)
        right = jnp.where(lat_ids == row, 1.0, 0.0).astype(jnp.bfloat16)
        wsum[...] += dot(left, right, NT)
        return carry

    chunks = cell.shape[1] // CHUNK
    early, late = chunks * 3 // 8, chunks * 5 // 8
    lax.fori_loop(0, early, weights, 0)

    for c in range(3):
        for i in range(1, na):
            for j in range(1, nb):
                sum0[i, j, c].wait_recv()
                stage[i * nb, c, halves[0]] += relay0[j - 1, i - 1, c]
            relayed0[i, c].start()
        for j in range(1, nb):
            for i in range(1, na):
                sum1[i, j, c].wait_recv()
                stage[j, c, halves[1]] += relay1[i - 1, j - 1, c]
            relayed1[j, c].start()

    lax.fori_loop(early, late, weights, 0)

    left_dev = (me_e, lax.rem(me_l + lon - 1, lon))
    right_dev = (me_e, lax.rem(me_l + 1, lon))

    def halo_copies(ref, which):
        return (
            remote(ref.at[which, pl.ds(HALO, HALO), :], ref.at[which, pl.ds(HALO + cols, HALO), :], left_dev),
            remote(ref.at[which, pl.ds(cols, HALO), :], ref.at[which, pl.ds(0, HALO), :], right_dev),
        )

    mine = lanes_of(me_e)
    own_a, own_b, pass_a, pass_b = {}, {}, {}, {}
    for c in range(3):
        whole = fields.at[c, pl.ds(HALO, cols), mine]
        for i in range(1, na):
            own_a[i, c] = remote(reduced.at[c], whole, a_peer(i))
        for j in range(1, nb):
            own_b[j, c] = remote(reduced.at[c], whole, b_peer(j))
        for i in range(1, na):
            for j in range(1, nb):
                from_b = lanes_of(me_a * nb + lax.rem(me_b + nb - j, nb))
                from_a = lanes_of(lax.rem(me_a + na - i, na) * nb + me_b)
                spot0 = fields.at[c, inner[0], from_b]
                spot1 = fields.at[c, inner[1], from_a]
                pass_a[i, j, c] = remote(spot0, spot0, a_peer(i))
                pass_b[i, j, c] = remote(spot1, spot1, b_peer(j))

    for c in range(3):
        total = stage[0, c]
        for j in range(1, nb):
            direct[0, j, c].wait_recv()
            relayed1[j, c].wait_recv()
            total = total + arr_b[j - 1, c]
        for i in range(1, na):
            direct[i, 0, c].wait_recv()
            relayed0[i, c].wait_recv()
            total = total + arr_a[i - 1, c]
        reduced[c] = total
        fields[c, pl.ds(HALO, cols), mine] = total
        for copy in [own_a[i, c] for i in range(1, na)] + [own_b[j, c] for j in range(1, nb)]:
            copy.start()
    lax.fori_loop(late, chunks, weights, 0)
    for s in range(STEPS):
        wmat[s, pl.ds(HALO, cols), :] = (
            wsum[pl.ds(s * cols, cols), :] + wsum[pl.ds(slots_cols + s * cols, cols), :]
        )

    w_copies = (
        remote(wmat.at[:, pl.ds(HALO, HALO), :], wmat.at[:, pl.ds(HALO + cols, HALO), :], left_dev),
        remote(wmat.at[:, pl.ds(cols, HALO), :], wmat.at[:, pl.ds(0, HALO), :], right_dev),
    )
    for copy in w_copies:
        copy.start()

    load_r.wait()
    for c in range(3):
        for j in range(1, nb):
            own_b[j, c].wait_recv()
            for i in range(1, na):
                pass_a[i, j, c].start()
        for i in range(1, na):
            own_a[i, c].wait_recv()
            for j in range(1, nb):
                pass_b[i, j, c].start()
    f_copies = []
    for c in range(3):
        for i in range(1, na):
            for j in range(1, nb):
                pass_a[i, j, c].wait_recv()
                pass_b[i, j, c].wait_recv()
        for copy in halo_copies(fields, c):
            copy.start()
            f_copies.append(copy)
    for group in (pass_a, pass_b):
        for copy in group.values():
            copy.wait_send()
    wide = fields.shape[1]
    every = range(0, wide, 8)

    def forward(source, target, n, blocks):
        linear_step(source, target, 1.0, consts, blocks)
        for start in blocks:
            heights[n, pl.ds(start, 8), :] = target[0, pl.ds(start, 8), :]

    inside = [range(HALO + 8 * (n + 1), wide - HALO - 8 * (n + 1), 8) for n in range(STEPS)]
    outer = [[start for start in every if start not in inside[n]] for n in range(STEPS)]
    buffers = (fields, other, fields, other)
    for n in range(STEPS):
        forward(buffers[n], buffers[n + 1], n, inside[n])
    for copy in f_copies:
        copy.wait()
    for n in range(STEPS):
        forward(buffers[n], buffers[n + 1], n, outer[n])
    for copy in w_copies:
        copy.wait()
    fields[0] = wmat[2] * heights[2]
    fields[1] = jnp.zeros_like(fields[1])
    fields[2] = jnp.zeros_like(fields[2])
    linear_step(fields, other, -1.0, consts, every)
    other[0] += wmat[1] * heights[1]
    linear_step(other, fields, -1.0, consts, every)
    fields[0] += wmat[0] * heights[0]
    linear_step(fields, other, -1.0, consts, every)

    for m in range(members):
        total = None
        for c in range(3):
            term = perturb[m, c].astype(jnp.float32) * other[c, pl.ds(HALO, cols), :]
            total = term if total is None else total + term
        p_high, p_low = split_bf16(total)
        split[pl.ds(m * cols, cols), :] = p_high
        split[pl.ds(stacked + m * cols, cols), :] = p_low

    def pulled(index, sums):
        at = lanes_of(index)
        both = dot(split[...], high[:, at], NN)
        back = both[:stacked] + both[stacked:] + dot(split[pl.ds(0, stacked), :], low[:, at], NN)
        out = []
        d = direction[:, :, at].reshape(stacked, block)
        r = residual[:, :, at].reshape(stacked, block)
        img = d + back
        image[:, :, at] = img.reshape(members, cols, block)
        for total, term in zip(sums, (r * r, d * img, r * img, img * img)):
            term = term.reshape(stacked // 8, 8, block).sum(axis=0)
            for k in range(block // 128):
                total = total + term[:, k * 128:(k + 1) * 128]
            out.append(total)
        return tuple(out)

    sums = lax.fori_loop(0, ens, pulled, tuple(jnp.zeros((8, 128), jnp.float32) for _ in range(4)))
    rows = [jnp.sum(s, axis=0, keepdims=True) for s in sums]
    lane = lax.broadcasted_iota(jnp.int32, (1, 128), 1) // 32
    packed = jnp.zeros((1, 128), jnp.float32)
    for k, row in enumerate(rows):
        row = row + pltpu.roll(row, 64, 1)
        row = row + pltpu.roll(row, 32, 1)
        packed = jnp.where(lane == k, row, packed)
    tile[...] = packed

    def tell(offset, carry):
        peer = lax.rem(me + offset, count)
        pltpu.make_async_remote_copy(
            src_ref=tile, dst_ref=tiles.at[offset - 1],
            send_sem=tile_send, recv_sem=tile_recv,
            device_id=(peer // lon, lax.rem(peer, lon)), device_id_type=MESH,
        ).start()
        return carry

    lax.fori_loop(1, count, tell, 0)
    for group in (sum0, sum1, direct, relayed0, relayed1, own_a, own_b):
        for copy in group.values():
            copy.wait_send()
    everything = pltpu.make_async_remote_copy(
        src_ref=tiles, dst_ref=tiles, send_sem=tile_send, recv_sem=tile_recv,
        device_id=right_dev, device_id_type=MESH,
    )
    everything.wait_send()
    everything.wait_recv()
    total = jnp.sum(tiles[...], axis=0) + tile[...]
    norm_old, curvature, cross_term, square = (
        jnp.sum(jnp.where(lane == k, total, 0.0), axis=1, keepdims=True) for k in range(4)
    )
    step_size = norm_old / curvature
    norm_new = norm_old - 2.0 * step_size * cross_term + step_size * step_size * square
    step_row[...] = jnp.broadcast_to(step_size, step_row.shape)
    ratio_row[...] = jnp.broadcast_to(norm_new / norm_old, ratio_row.shape)


def body(ens, lon, control, residual, direction, ens_perturb, localize, obs_cell, obs_slot, obs_weight):
    flip = functools.partial(jnp.swapaxes, axis1=-1, axis2=-2)
    control, residual, direction, ens_perturb = map(flip, (control, residual, direction, ens_perturb))
    members, cols, lat = direction.shape
    nobs = obs_cell.shape[0]
    block = lat // ens
    na, nb = factors(ens)
    pa, pb = max(na - 1, 1), max(nb - 1, 1)
    count = ens * lon
    wide = cols + 2 * HALO
    f32, bf16 = jnp.float32, jnp.bfloat16
    vmem = pl.BlockSpec(memory_space=pltpu.VMEM)
    outside = pl.BlockSpec(memory_space=pl.ANY)
    dma = pltpu.SemaphoreType.DMA
    row = jax.ShapeDtypeStruct((1, lat), f32)
    image, step_size, ratio = pl.pallas_call(
        functools.partial(kernel, ens, lon),
        out_shape=(jax.ShapeDtypeStruct((members, cols, lat), f32), row, row),
        in_specs=[vmem, outside, outside, outside] + [vmem] * 4,
        out_specs=(vmem, vmem, vmem),
        scratch_shapes=[
            pltpu.VMEM((lat, lat), f32),
            pltpu.VMEM((members, cols, lat), f32),
            pltpu.VMEM((members, 3, cols, lat), bf16),
            pltpu.VMEM((lat, lat), bf16),
            pltpu.VMEM((lat, lat), bf16),
            pltpu.VMEM((2 * members * cols, lat), bf16),
            pltpu.VMEM((ens, 3, cols, block), f32),
            pltpu.VMEM((pb, pa, 3, cols // 2, block), f32),
            pltpu.VMEM((pa, pb, 3, cols // 2, block), f32),
            pltpu.VMEM((pa, 3, cols, block), f32),
            pltpu.VMEM((pb, 3, cols, block), f32),
            pltpu.VMEM((3, cols, block), f32),
            pltpu.VMEM((3, wide, lat), f32),
            pltpu.VMEM((3, wide, lat), f32),
            pltpu.VMEM((STEPS, wide, lat), f32),
            pltpu.VMEM((2 * STEPS * cols, lat), f32),
            pltpu.VMEM((STEPS, wide, lat), f32),
            pltpu.VMEM((count - 1, 1, 128), f32),
            pltpu.VMEM((1, 128), f32),
            dma((ens + 2,)), dma((copy_count(ens),)), dma((copy_count(ens),)),
            dma, dma,
        ],
        compiler_params=pltpu.CompilerParams(collective_id=0, has_side_effects=True),
    )(
        direction, residual, ens_perturb, localize,
        obs_cell.reshape(1, nobs), obs_slot.reshape(1, nobs), obs_weight.reshape(1, nobs),
        jnp.asarray(grid_constants(lat)),
    )
    control_new = control + step_size * direction
    residual_new = residual - step_size * image
    direction_new = residual_new + ratio * direction
    return tuple(map(flip, (control_new, residual_new, direction_new)))


def solution(mesh):
    fields = P("ens", None, "lon")
    in_specs = (fields, fields, fields, P("ens", None, None, "lon"), P(), P("lon"), P("lon"), P("lon"))
    ens, lon = mesh.shape["ens"], mesh.shape["lon"]
    return jax.shard_map(
        functools.partial(body, ens, lon), mesh=mesh, in_specs=in_specs,
        out_specs=(fields, fields, fields), check_vma=False,
    )
```

profile of v0, /device:TPU:0, one launch (start us, length us, event | category | flops | bytes accessed | tf_op | source)
XLA Modules:
  0.0 42.1 jit_solution(3214842533975065316)
XLA Ops:
  0.6 0.0 copy-start
  0.6 0.0 copy-start.1
  0.7 0.0 copy-start.2
  0.7 37.7 %shard_map.112 = (f32[2,64,1024]{2,1,0:T(8,128)}, f32[1,1024]{1,0:T(1,128)}, f32[1,1024]{1,0:T(1,128)}) custom-call(f32[2,64,1024]{2,1,0:T(8,128)} %bitcast.15, f32[2,64,1024]{2,1,0:T(8,128)} %bitcast.16, bf16[2,3,64,1024]{3,2,1,0:T(8,128)(2,1)} %bitcast.17, f32[1024,1024]{1,0:T(8,128)} %localize_hbm.1, s32[1,4096]{1,0:T(1,128)} %bitcast.18, ...), custom_call_target="tpu_custom_call" | custom-call | tf_op jit(solution)/shard_map/pallas_call | solution.py:414
  38.4 0.0 copy-done
  38.4 0.0 copy-done.1
  38.4 2.2 %add_bitcast_fusion = (f32[2,1024,64]{1,2,0:T(8,128)}, f32[2,1024,64]{1,2,0:T(8,128)}) fusion(f32[1024]{0:T(1024)} %bitcast.23, f32[2,64,1024]{2,1,0:T(8,128)} %get-tuple-element.7, f32[1024]{0:T(1024)} %bitcast.21, f32[2,1024,64]{1,2,0:T(8,128)S(1)} %copy-done.1, f32[2,1024,64]{1,2,0:T(8,128)S(1)} %copy-done), kind=kLoop, calls=%fused_computation | loop fusion | flops 524288 | bytes 2629632 | tf_op jit(solution)/shard_map/transpose | solution.py:451
  40.6 0.0 copy-done.2
  40.6 1.5 %multiply_add_fusion = f32[2,1024,64]{1,2,0:T(8,128)} fusion(f32[2,1024,64]{1,2,0:T(8,128)S(1)} %copy-done.2, f32[2,1024,64]{1,2,0:T(8,128)S(1)} %copy-done, f32[1024]{0:T(1024)} %bitcast.22), kind=kLoop, calls=%fused_computation.2 | loop fusion | flops 262144 | bytes 1576960 | tf_op jit(solution)/shard_map/add | solution.py:448
Async XLA Ops:
  0.6 37.8 %copy-start = (f32[2,1024,64]{1,2,0:T(8,128)S(1)}, f32[2,1024,64]{1,2,0:T(8,128)}, u32[]{:S(2)}) copy-start(f32[2,1024,64]{1,2,0:T(8,128)} %param.11) | copy-start | bytes 1572868
  0.6 37.8 %copy-start.1 = (f32[2,1024,64]{1,2,0:T(8,128)S(1)}, f32[2,1024,64]{1,2,0:T(8,128)}, u32[]{:S(2)}) copy-start(f32[2,1024,64]{1,2,0:T(8,128)} %param.10) | copy-start | bytes 1572868
  0.7 40.0 %copy-start.2 = (f32[2,1024,64]{1,2,0:T(8,128)S(1)}, f32[2,1024,64]{1,2,0:T(8,128)}, u32[]{:S(2)}) copy-start(f32[2,1024,64]{1,2,0:T(8,128)} %param.9) | copy-start | bytes 1572868
where the time goes:
time: 42.3 us; the launch traced here: 42.1 us
  Pallas kernels  37.7 us (89%)
  other arithmetic  3.7 us (9%)
  between operations  0.68 us (2%)
    pallas_call x1, Pallas kernels, body(): pl.pallas_call(functools.partial(kernel, ens, lon), out_shape=(jax.ShapeD...  37.7 us
    transpose x1, other arithmetic, body(): return tuple(map(flip, (control_new, residual_new, direction_new)))  2.17 us
    add x1, other arithmetic, body(): control_new = control + step_size * direction  1.54 us

commit v1 on v0

v1 whole, which is shorter than its diff:
```python
import functools
import itertools

import numpy as np
import jax
import jax.numpy as jnp
from jax import lax
from jax.experimental import pallas as pl
from jax.experimental.pallas import tpu as pltpu
from jax.sharding import PartitionSpec as P

STEPS = 3
HALO = 8
CHUNK = 1024
BLOCK = 256
MESH = pl.DeviceIdType.MESH
NT = (((1,), (1,)), ((), ()))
NN = (((1,), (0,)), ((), ()))


def split_bf16(values):
    high = values.astype(jnp.bfloat16)
    low = (values - high.astype(jnp.float32)).astype(jnp.bfloat16)
    return high, low


def dot(left, right, dims):
    return lax.dot_general(left, right, dims, preferred_element_type=jnp.float32)


def grid_constants(lat):
    phi = np.pi * (-1.0 / 3.0 + 2.0 / 3.0 * (np.arange(lat) + 0.5) / lat)
    half = 0.5 * 0.35
    up = np.full(lat, half)
    up[-1] = 0.0
    down = np.full(lat, half)
    down[0] = 0.0
    rows = np.stack([half / np.cos(phi), 0.2 * np.sin(phi), up, down])
    return np.ascontiguousarray(np.broadcast_to(rows[:, None], (4, 8, lat))).astype(np.float32)


def linear_step(source, target, sign, consts, blocks):
    rows, lat = source.shape[1], source.shape[2]
    lon_c, cor_c, up_c, down_c = (sign * consts[k] for k in range(4))
    for start in blocks:
        here = pl.ds(start, 8)

        def east(comp, block):
            if start + 8 == rows:
                return pltpu.roll(block, 7, 0)
            return source[comp, pl.ds(start + 1, 8), :]

        def west(comp, block):
            if start == 0:
                return pltpu.roll(block, 1, 0)
            return source[comp, pl.ds(start - 1, 8), :]

        def lat_diff(block):
            return up_c * pltpu.roll(block, lat - 1, 1) - down_c * pltpu.roll(block, 1, 1)

        height, zonal, merid = (source[c, here, :] for c in range(3))
        height_lon = east(0, height) - west(0, height)
        zonal_lon = east(1, zonal) - west(1, zonal)
        target[0, here, :] = height - lon_c * zonal_lon - lat_diff(merid)
        target[1, here, :] = zonal - lon_c * height_lon + cor_c * merid
        target[2, here, :] = merid - lat_diff(height) - cor_c * zonal


def grid_blocks(total, size):
    return range(0, total, size)


def row16(values):
    return jnp.broadcast_to(values, (16, values.shape[1])).astype(jnp.bfloat16)


def fold(values):
    values = values + pltpu.roll(values, 64, 1)
    return values + pltpu.roll(values, 32, 1)


def pack_rows(rows):
    lane = lax.broadcasted_iota(jnp.int32, (1, 128), 1) // 32
    packed = jnp.zeros((1, 128), jnp.float32)
    for k, row in enumerate(rows):
        packed = jnp.where(lane == k, fold(row), packed)
    return packed


def unpack_rows(total, number):
    lane = lax.broadcasted_iota(jnp.int32, (1, 128), 1) // 32
    return [
        jnp.sum(jnp.where(lane == k, total, 0.0), axis=1, keepdims=True) for k in range(number)
    ]


def lane_sum(values):
    total = values[:, :128]
    for k in range(128, values.shape[1], 128):
        total = total + values[:, k:k + 128]
    return total


def remote_count(ens, lat, nobs):
    return 2 * (lat // BLOCK) + (ens - 1) * (nobs // CHUNK) + 2 * STEPS


def kernel(
    ens, lon, direction_hbm, residual_hbm, perturb_hbm, localize_hbm, cell_hbm, slot_hbm,
    weight_hbm, consts_hbm,
    image, step_row, ratio_row,
    direction, localize, residual, perturb, cell, slot, weight, consts,
    high, low, split, onehot, fields, other, heights, observed, arrived, spread, forcing,
    tiles, tile, tiles2, tile2,
    load_sem, send_sem, recv_sem, tile_send, tile_recv, tile2_send, tile2_recv,
):
    me_e, me_l = lax.axis_index("ens"), lax.axis_index("lon")
    count = ens * lon
    me = me_e * lon + me_l
    members, cols, lat = direction.shape
    nobs = cell.shape[1]
    stacked = members * cols
    slots_cols = STEPS * cols
    blocks = [pl.ds(k, BLOCK) for k in grid_blocks(lat, BLOCK)]
    chunks = [pl.ds(k, CHUNK) for k in grid_blocks(nobs, CHUNK)]
    left_dev = (me_e, lax.rem(me_l + lon - 1, lon))
    right_dev = (me_e, lax.rem(me_l + 1, lon))

    load_ids = itertools.count()

    def load(src, dst):
        copy = pltpu.make_async_copy(src, dst, load_sem.at[next(load_ids)])
        copy.start()
        return copy

    load_obs = [load(cell_hbm, cell), load(slot_hbm, slot), load(weight_hbm, weight)]
    load_d = load(direction_hbm, direction)
    load_l = [load(localize_hbm.at[at, :], localize.at[at, :]) for at in blocks]
    load_p = load(perturb_hbm, perturb)
    load_c = load(consts_hbm, consts)
    load_r = load(residual_hbm, residual)

    barrier = pltpu.get_barrier_semaphore()

    def greet(offset, carry):
        peer = lax.rem(me + offset, count)
        pl.semaphore_signal(
            barrier, inc=1, device_id=(peer // lon, lax.rem(peer, lon)), device_id_type=MESH
        )
        return carry

    lax.fori_loop(1, count, greet, 0)

    ids = itertools.count()

    def remote(src, dst, device):
        k = next(ids)
        return pltpu.make_async_remote_copy(
            src_ref=src, dst_ref=dst, send_sem=send_sem.at[k], recv_sem=recv_sem.at[k],
            device_id=device, device_id_type=MESH,
        )

    def tell_all(source, target, send, recv):
        def tell(offset, carry):
            peer = lax.rem(me + offset, count)
            pltpu.make_async_remote_copy(
                src_ref=source, dst_ref=target.at[offset - 1], send_sem=send, recv_sem=recv,
                device_id=(peer // lon, lax.rem(peer, lon)), device_id_type=MESH,
            ).start()
            return carry

        lax.fori_loop(1, count, tell, 0)

    def hear_all(target, send, recv):
        everything = pltpu.make_async_remote_copy(
            src_ref=target, dst_ref=target, send_sem=send, recv_sem=recv,
            device_id=right_dev, device_id_type=MESH,
        )
        everything.wait_send()
        everything.wait_recv()

    for copy in load_obs:
        copy.wait()
    ids16 = lax.broadcasted_iota(jnp.int32, (16, 128), 0).astype(jnp.float32)
    tags = [(ids16 + 16.0 * g).astype(jnp.bfloat16) for g in range(BLOCK // 16)]
    one, zero = jnp.ones((16, 128), jnp.bfloat16), jnp.zeros((16, 128), jnp.bfloat16)

    def mark(step, carry):
        at = pl.ds(pl.multiple_of(step * 128, 128), 128)
        row = cell[:, at] // cols
        for b in grid_blocks(lat, BLOCK):
            inside = (row >= b) & (row < b + BLOCK)
            here = row16(jnp.where(inside, row - b, -1).astype(jnp.float32))
            for g in range(BLOCK // 16):
                onehot[pl.ds(b + 16 * g, 16), at] = jnp.where(here == tags[g], one, zero)
        return carry

    lax.fori_loop(0, nobs // 128, mark, 0)

    load_d.wait()
    d_high, d_low = split_bf16(direction[...].reshape(stacked, lat))
    split[pl.ds(0, stacked), :] = d_high
    split[pl.ds(stacked, stacked), :] = d_low

    edge = STEPS
    own = pl.ds(HALO, cols)
    first, last = pl.ds(HALO, edge), pl.ds(HALO + cols - edge, edge)
    before, after = pl.ds(HALO - edge, edge), pl.ds(HALO + cols, edge)

    def halo(ref, which, at):
        return (
            remote(ref.at[which, first, at], ref.at[which, after, at], left_dev),
            remote(ref.at[which, last, at], ref.at[which, before, at], right_dev),
        )

    f_copies = []
    for k, at in enumerate(blocks):
        load_l[k].wait()
        l_high, l_low = split_bf16(localize[at, :])
        high[at, :] = l_high
        low[at, :] = l_low
        both = dot(split[...], l_high, NT)
        local = both[:stacked] + both[stacked:] + dot(split[pl.ds(0, stacked), :], l_low, NT)
        if k == 0:
            load_p.wait()
        for c in range(3):
            total = None
            for m in range(members):
                term = perturb[m, c, :, at].astype(jnp.float32) * local[m * cols:(m + 1) * cols]
                total = term if total is None else total + term
            fields[c, own, at] = total
        if k == 0:
            pl.semaphore_wait(barrier, count - 1)
        for copy in halo(fields, pl.ds(0, 3), at):
            copy.start()
            f_copies.append(copy)

    load_c.wait()
    wide = fields.shape[1]

    def forward(source, target, n, blocks):
        linear_step(source, target, 1.0, consts, blocks)
        for start in blocks:
            if HALO <= start < HALO + cols:
                value = target[0, pl.ds(start, 8), :]
                v_high = value.astype(jnp.bfloat16).astype(jnp.float32)
                heights[pl.ds(n * cols + start - HALO, 8), :] = v_high
                heights[pl.ds(slots_cols + n * cols + start - HALO, 8), :] = value - v_high

    every = range(0, wide, 8)
    inside = [range(HALO + 8 * (n + 1), wide - HALO - 8 * (n + 1), 8) for n in range(STEPS)]
    outer = [[start for start in every if start not in inside[n]] for n in range(STEPS)]
    buffers = (fields, other, fields, other)
    for copy in f_copies:
        copy.wait_send()
    for n in range(STEPS):
        forward(buffers[n], buffers[n + 1], n, inside[n])

    load_r.wait()
    norms = [jnp.zeros((8, 128), jnp.float32)] * 2
    for at in blocks:
        for j, ref in enumerate((residual, direction)):
            value = ref[:, :, at]
            value = (value * value).reshape(stacked // 8, 8, BLOCK).sum(axis=0)
            norms[j] = norms[j] + lane_sum(value)
    norms = [jnp.sum(value, axis=0, keepdims=True) for value in norms]

    for copy in f_copies:
        copy.wait_recv()
    for n in range(STEPS):
        forward(buffers[n], buffers[n + 1], n, outer[n])

    def keys(at):
        cells, slots = cell[:, at], slot[:, at]
        return slots * cols + (cells - cells // cols * cols)

    peers = [(lax.rem(me_e + k, ens), me_l) for k in range(1, ens)]
    sums = {}
    table = heights[...].astype(jnp.bfloat16)
    key_ids = lax.broadcasted_iota(jnp.int32, (slots_cols, CHUNK), 0)
    for k, at in enumerate(chunks):
        both = dot(table, onehot[:, at], NN)
        both = both[:slots_cols] + both[slots_cols:]
        picked = jnp.where(key_ids == keys(at), both, 0.0)
        observed[:, at] = jnp.sum(picked, axis=0, keepdims=True)
        for j, peer in enumerate(peers):
            sums[j, k] = remote(observed.at[:, at], arrived.at[j, :, at], peer)
            sums[j, k].start()

    misfit = jnp.zeros((1, 128), jnp.float32)
    for k, at in enumerate(chunks):
        total = observed[:, at]
        for j in range(ens - 1):
            sums[j, k].wait_recv()
            total = total + arrived[j, :, at]
        weighted = weight[:, at] * total
        misfit = misfit + lane_sum(jnp.where(slot[:, at] < STEPS, weighted * total, 0.0))
        w_high = weighted.astype(jnp.bfloat16).astype(jnp.float32)
        w_low = weighted - w_high
        hit = key_ids == keys(at)
        left = jnp.concatenate(
            [jnp.where(hit, w_high, 0.0), jnp.where(hit, w_low, 0.0)], axis=0
        ).astype(jnp.bfloat16)
        both = dot(left, onehot[:, at], NT)
        both = both[:slots_cols] + both[slots_cols:]
        if k == 0:
            spread[...] = both
        else:
            spread[...] += both

    tile[...] = pack_rows([norms[0], norms[1], misfit * (1.0 / ens)])
    tell_all(tile, tiles, tile_send, tile_recv)

    for s in range(STEPS):
        forcing[s, own, :] = spread[pl.ds(s * cols, cols), :]
    w_copies = []
    for s in range(STEPS):
        for copy in halo(forcing, s, pl.ds(0, lat)):
            copy.start()
            w_copies.append(copy)

    for copy in w_copies:
        copy.wait()
    fields[0] = forcing[2]
    fields[1] = jnp.zeros_like(fields[1])
    fields[2] = jnp.zeros_like(fields[2])
    linear_step(fields, other, -1.0, consts, every)
    other[0] += forcing[1]
    linear_step(other, fields, -1.0, consts, every)
    fields[0] += forcing[0]
    linear_step(fields, other, -1.0, consts, every)

    for m in range(members):
        total = None
        for c in range(3):
            term = perturb[m, c].astype(jnp.float32) * other[c, own, :]
            total = term if total is None else total + term
        p_high, p_low = split_bf16(total)
        split[pl.ds(m * cols, cols), :] = p_high
        split[pl.ds(stacked + m * cols, cols), :] = p_low

    hear_all(tiles, tile_send, tile_recv)
    norm_old, square, misfit = unpack_rows(jnp.sum(tiles[...], axis=0) + tile[...], 3)
    step_size = norm_old / (square + misfit)

    def pulled(index, total):
        at = pl.ds(pl.multiple_of(index * BLOCK, BLOCK), BLOCK)
        both = dot(split[...], high[:, at], NN)
        back = both[:stacked] + both[stacked:] + dot(split[pl.ds(0, stacked), :], low[:, at], NN)
        d = direction[:, :, at].reshape(stacked, BLOCK)
        r = residual[:, :, at].reshape(stacked, BLOCK)
        img = d + back
        image[:, :, at] = img.reshape(members, cols, BLOCK)
        new = r - step_size * img
        return total + lane_sum((new * new).reshape(stacked // 8, 8, BLOCK).sum(axis=0))

    norm_new = lax.fori_loop(0, lat // BLOCK, pulled, jnp.zeros((8, 128), jnp.float32))
    tile2[...] = pack_rows([jnp.sum(norm_new, axis=0, keepdims=True)])
    tell_all(tile2, tiles2, tile2_send, tile2_recv)
    for copy in sums.values():
        copy.wait_send()
    hear_all(tiles2, tile2_send, tile2_recv)
    (norm_new,) = unpack_rows(jnp.sum(tiles2[...], axis=0) + tile2[...], 1)
    step_row[...] = jnp.broadcast_to(step_size, step_row.shape)
    ratio_row[...] = jnp.broadcast_to(norm_new / norm_old, ratio_row.shape)


def body(ens, lon, control, residual, direction, ens_perturb, localize, obs_cell, obs_slot, obs_weight):
    flip = functools.partial(jnp.swapaxes, axis1=-1, axis2=-2)
    control, residual, direction, ens_perturb = map(flip, (control, residual, direction, ens_perturb))
    members, cols, lat = direction.shape
    nobs = obs_cell.shape[0]
    count = ens * lon
    wide = cols + 2 * HALO
    f32, bf16, i32 = jnp.float32, jnp.bfloat16, jnp.int32
    vmem = pl.BlockSpec(memory_space=pltpu.VMEM)
    outside = pl.BlockSpec(memory_space=pl.ANY)
    dma = pltpu.SemaphoreType.DMA
    row = jax.ShapeDtypeStruct((1, lat), f32)
    copies = remote_count(ens, lat, nobs)
    image, step_size, ratio = pl.pallas_call(
        functools.partial(kernel, ens, lon),
        out_shape=(jax.ShapeDtypeStruct((members, cols, lat), f32), row, row),
        in_specs=[outside] * 8,
        out_specs=(vmem, vmem, vmem),
        scratch_shapes=[
            pltpu.VMEM((members, cols, lat), f32),
            pltpu.VMEM((lat, lat), f32),
            pltpu.VMEM((members, cols, lat), f32),
            pltpu.VMEM((members, 3, cols, lat), bf16),
            pltpu.VMEM((1, nobs), i32),
            pltpu.VMEM((1, nobs), i32),
            pltpu.VMEM((1, nobs), f32),
            pltpu.VMEM((4, 8, lat), f32),
            pltpu.VMEM((lat, lat), bf16),
            pltpu.VMEM((lat, lat), bf16),
            pltpu.VMEM((2 * members * cols, lat), bf16),
            pltpu.VMEM((lat, nobs), bf16),
            pltpu.VMEM((3, wide, lat), f32),
            pltpu.VMEM((3, wide, lat), f32),
            pltpu.VMEM((2 * STEPS * cols, lat), f32),
            pltpu.VMEM((1, nobs), f32),
            pltpu.VMEM((max(ens - 1, 1), 1, nobs), f32),
            pltpu.VMEM((STEPS * cols, lat), f32),
            pltpu.VMEM((STEPS, wide, lat), f32),
            pltpu.VMEM((count - 1, 1, 128), f32),
            pltpu.VMEM((1, 128), f32),
            pltpu.VMEM((count - 1, 1, 128), f32),
            pltpu.VMEM((1, 128), f32),
            dma((7 + lat // BLOCK,)), dma((copies,)), dma((copies,)),
            dma, dma, dma, dma,
        ],
        compiler_params=pltpu.CompilerParams(collective_id=0, has_side_effects=True),
    )(
        direction, residual, ens_perturb, localize,
        obs_cell.reshape(1, nobs), obs_slot.reshape(1, nobs), obs_weight.reshape(1, nobs),
        jnp.asarray(grid_constants(lat)),
    )
    control_new = control + step_size * direction
    residual_new = residual - step_size * image
    direction_new = residual_new + ratio * direction
    return tuple(map(flip, (control_new, residual_new, direction_new)))


def solution(mesh):
    fields = P("ens", None, "lon")
    in_specs = (fields, fields, fields, P("ens", None, None, "lon"), P(), P("lon"), P("lon"), P("lon"))
    ens, lon = mesh.shape["ens"], mesh.shape["lon"]
    return jax.shard_map(
        functools.partial(body, ens, lon), mesh=mesh, in_specs=in_specs,
        out_specs=(fields, fields, fields), check_vma=False,
    )
```

time: 42.3 us -> 39.2 us (0.927)
  Pallas kernels: 37.7 us -> 34.6 us
    pallas_call x1, Pallas kernels: 37.7 us -> 34.6 us  [body(): pl.pallas_call(functools.partial(kernel, ens, lon), out_shape=(jax.ShapeD...]
where the time goes in v1:
time: 39.2 us; the launch traced here: 39 us
  Pallas kernels  34.6 us (88%)
  other arithmetic  3.7 us (9%)
  between operations  0.68 us (2%)
    pallas_call x1, Pallas kernels, body(): pl.pallas_call(functools.partial(kernel, ens, lon), out_shape=(jax.ShapeD...  34.6 us
    transpose x1, other arithmetic, body(): return tuple(map(flip, (control_new, residual_new, direction_new)))  2.17 us
    add x1, other arithmetic, body(): control_new = control + step_size * direction  1.54 us

profile of v1, /device:TPU:0, one launch (start us, length us, event | category | flops | bytes accessed | tf_op | source)
XLA Modules:
  0.0 39.0 jit_solution(13435577128714136514)
XLA Ops:
  0.6 0.0 copy-start
  0.6 0.0 copy-start.1
  0.7 0.0 copy-start.2
  0.7 34.6 %shard_map.112 = (f32[2,64,1024]{2,1,0:T(8,128)}, f32[1,1024]{1,0:T(1,128)}, f32[1,1024]{1,0:T(1,128)}) custom-call(f32[2,64,1024]{2,1,0:T(8,128)} %bitcast.15, f32[2,64,1024]{2,1,0:T(8,128)} %bitcast.16, bf16[2,3,64,1024]{3,2,1,0:T(8,128)(2,1)} %bitcast.17, f32[1024,1024]{1,0:T(8,128)} %localize_hbm.1, s32[1,4096]{1,0:T(1,128)} %bitcast.18, ...), custom_call_target="tpu_custom_call" | custom-call | tf_op jit(solution)/shard_map/pallas_call | solution.py:381
  35.3 0.0 copy-done
  35.3 0.0 copy-done.1
  35.3 2.2 %add_bitcast_fusion = (f32[2,1024,64]{1,2,0:T(8,128)}, f32[2,1024,64]{1,2,0:T(8,128)}) fusion(f32[1024]{0:T(1024)} %bitcast.23, f32[2,64,1024]{2,1,0:T(8,128)} %get-tuple-element.7, f32[1024]{0:T(1024)} %bitcast.21, f32[2,1024,64]{1,2,0:T(8,128)S(1)} %copy-done.1, f32[2,1024,64]{1,2,0:T(8,128)S(1)} %copy-done), kind=kLoop, calls=%fused_computation | loop fusion | flops 524288 | bytes 2629632 | tf_op jit(solution)/shard_map/transpose | solution.py:422
  37.5 0.0 copy-done.2
  37.5 1.5 %multiply_add_fusion = f32[2,1024,64]{1,2,0:T(8,128)} fusion(f32[2,1024,64]{1,2,0:T(8,128)S(1)} %copy-done.2, f32[2,1024,64]{1,2,0:T(8,128)S(1)} %copy-done, f32[1024]{0:T(1024)} %bitcast.22), kind=kLoop, calls=%fused_computation.2 | loop fusion | flops 262144 | bytes 1576960 | tf_op jit(solution)/shard_map/add | solution.py:419
Async XLA Ops:
  0.6 34.7 %copy-start = (f32[2,1024,64]{1,2,0:T(8,128)S(1)}, f32[2,1024,64]{1,2,0:T(8,128)}, u32[]{:S(2)}) copy-start(f32[2,1024,64]{1,2,0:T(8,128)} %param.11) | copy-start | bytes 1572868
  0.6 34.7 %copy-start.1 = (f32[2,1024,64]{1,2,0:T(8,128)S(1)}, f32[2,1024,64]{1,2,0:T(8,128)}, u32[]{:S(2)}) copy-start(f32[2,1024,64]{1,2,0:T(8,128)} %param.10) | copy-start | bytes 1572868
  0.7 36.8 %copy-start.2 = (f32[2,1024,64]{1,2,0:T(8,128)S(1)}, f32[2,1024,64]{1,2,0:T(8,128)}, u32[]{:S(2)}) copy-start(f32[2,1024,64]{1,2,0:T(8,128)} %param.9) | copy-start | bytes 1572868

commit v2 on v1

v2 whole, which is shorter than its diff:
```python
import functools
import itertools

import numpy as np
import jax
import jax.numpy as jnp
from jax import lax
from jax.experimental import pallas as pl
from jax.experimental.pallas import tpu as pltpu
from jax.sharding import PartitionSpec as P

STEPS = 3
HALO = 8
CHUNK = 2048
BLOCK = 256
MESH = pl.DeviceIdType.MESH
NT = (((1,), (1,)), ((), ()))
NN = (((1,), (0,)), ((), ()))


def split_bf16(values):
    high = values.astype(jnp.bfloat16)
    low = (values - high.astype(jnp.float32)).astype(jnp.bfloat16)
    return high, low


def dot(left, right, dims):
    return lax.dot_general(left, right, dims, preferred_element_type=jnp.float32)


def grid_constants(lat):
    phi = np.pi * (-1.0 / 3.0 + 2.0 / 3.0 * (np.arange(lat) + 0.5) / lat)
    half = 0.5 * 0.35
    up = np.full(lat, half)
    up[-1] = 0.0
    down = np.full(lat, half)
    down[0] = 0.0
    rows = np.stack([half / np.cos(phi), 0.2 * np.sin(phi), up, down])
    return np.ascontiguousarray(np.broadcast_to(rows[:, None], (4, 8, lat))).astype(np.float32)


def linear_step(source, target, sign, consts, blocks, low_end, high_end, rest=True, extra=None):
    lat = source.shape[2]
    lon_c, cor_c, up_c, down_c = (consts[k] for k in range(4))

    def less(value, term):
        return value - term if sign > 0 else value + term

    for start in blocks:
        here = pl.ds(start, 8)

        def lon_diff(comp, block):
            if start + 8 == high_end:
                east = pltpu.roll(block, 7, 0)
            else:
                east = source[comp, pl.ds(start + 1, 8), :]
            if start == low_end:
                west = pltpu.roll(block, 1, 0)
            else:
                west = source[comp, pl.ds(start - 1, 8), :]
            return lon_c * (east - west)

        def lat_diff(block):
            return up_c * pltpu.roll(block, lat - 1, 1) - down_c * pltpu.roll(block, 1, 1)

        height = source[0, here, :]
        along_lon, along_lat = lon_diff(0, height), lat_diff(height)
        if rest:
            zonal, merid = source[1, here, :], source[2, here, :]
            new = less(height, lon_diff(1, zonal) + lat_diff(merid))
            target[1, here, :] = less(zonal, along_lon - cor_c * merid)
            target[2, here, :] = less(merid, along_lat + cor_c * zonal)
        else:
            new = height
            target[1, here, :] = less(0.0, along_lon)
            target[2, here, :] = less(0.0, along_lat)
        target[0, here, :] = new if extra is None else new + extra[here, :]


def fold(values):
    values = values + pltpu.roll(values, 64, 1)
    return values + pltpu.roll(values, 32, 1)


def pack_rows(rows):
    lane = lax.broadcasted_iota(jnp.int32, (1, 128), 1) // 32
    packed = jnp.zeros((1, 128), jnp.float32)
    for k, row in enumerate(rows):
        packed = jnp.where(lane == k, fold(row), packed)
    return packed


def unpack_rows(total, number):
    lane = lax.broadcasted_iota(jnp.int32, (1, 128), 1) // 32
    return [
        jnp.sum(jnp.where(lane == k, total, 0.0), axis=1, keepdims=True) for k in range(number)
    ]


def lane_sum(values):
    total = values[:, :128]
    for k in range(128, values.shape[1], 128):
        total = total + values[:, k:k + 128]
    return total


def remote_count(ens, lat, nobs):
    return 4 + (ens - 1) * (1 + nobs // CHUNK)


def side_rows():
    return [(n, k) for n in reversed(range(STEPS)) for k in range(n + 1)]


def kernel(
    ens, lon, control_hbm, direction_hbm, residual_hbm, perturb_hbm, localize_hbm, cell_hbm,
    slot_hbm, weight_hbm, consts_hbm,
    control, residual, direction, image, scalars,
    localize, perturb, cell, slot, weight, consts,
    high, low, split, onehot, state0, state1, state2, state3, heights, observed, arrived,
    spread, forcing, near, near_in, mass, mass_in, tiles, tile,
    load_sem, send_sem, recv_sem, tile_send, tile_recv,
):
    me_e, me_l = lax.axis_index("ens"), lax.axis_index("lon")
    members, cols, lat = direction.shape
    nobs = cell.shape[1]
    wide = state0.shape[1]
    stacked = members * cols
    slots_cols = STEPS * cols
    blocks = [pl.ds(k, BLOCK) for k in range(0, lat, BLOCK)]
    chunks = [pl.ds(k, CHUNK) for k in range(0, nobs, CHUNK)]
    panels = range(lat // 128)

    def wrap(value, size):
        return jnp.where(value >= size, value - size, value)

    left_dev = (me_e, wrap(me_l + lon - 1, lon))
    right_dev = (me_e, wrap(me_l + 1, lon))

    load_ids = itertools.count()

    def load(src, dst):
        copy = pltpu.make_async_copy(src, dst, load_sem.at[next(load_ids)])
        copy.start()
        return copy

    load_obs = [load(cell_hbm, cell), load(slot_hbm, slot), load(weight_hbm, weight)]
    load_d = load(direction_hbm, direction)
    load_l = [load(localize_hbm.at[at, :], localize.at[at, :]) for at in blocks]
    load_p = load(perturb_hbm, perturb)
    load_c = load(consts_hbm, consts)
    load_r = load(residual_hbm, residual)
    load_v = load(control_hbm, control)

    barrier = pltpu.get_barrier_semaphore()
    ids = itertools.count()

    def remote(src, dst, device):
        k = next(ids)
        return pltpu.make_async_remote_copy(
            src_ref=src, dst_ref=dst, send_sem=send_sem.at[k], recv_sem=recv_sem.at[k],
            device_id=device, device_id_type=MESH,
        )

    def each_peer(act):
        for e in range(ens):
            peer_e = wrap(me_e + e, ens)

            def visit(l, carry):
                act(e * lon + l - 1, (peer_e, wrap(me_l + l, lon)))
                return carry

            lax.fori_loop(0 if e else 1, lon, visit, 0, unroll=True)

    each_peer(lambda index, device: pl.semaphore_signal(
        barrier, inc=1, device_id=device, device_id_type=MESH
    ))

    for copy in load_obs:
        copy.wait()
    rows = (cell[...] // cols).reshape(nobs // 128, 128)
    rows = jnp.concatenate([rows] * (128 * 128 // nobs), axis=0).T
    lanes = lax.broadcasted_iota(jnp.int32, (16, 128), 1).astype(jnp.int16)
    one, zero = jnp.ones((16, 128), jnp.bfloat16), jnp.zeros((16, 128), jnp.bfloat16)
    for group in range(nobs // 128):
        for s in range(0, 128, 16):
            row = jnp.broadcast_to(rows[s:s + 16, group:group + 1], (16, 128)).astype(jnp.int16)
            for j in panels:
                hit = row == lanes + jnp.int16(128 * j)
                onehot[j, pl.ds(128 * group + s, 16), :] = jnp.where(hit, one, zero)

    def panel(ref, at, which=panels):
        return jnp.concatenate([ref[j, at, :] for j in which], axis=1)

    def store_panels(ref, at, values):
        for j in panels:
            ref[j, at, :] = values[:, 128 * j:128 * j + 128]

    load_d.wait()
    d_high, d_low = split_bf16(direction[...].reshape(stacked, lat))

    edge = 2 * STEPS
    own = pl.ds(HALO, cols)
    first, last = pl.ds(HALO, edge), pl.ds(HALO + cols - edge, edge)
    before, after = pl.ds(HALO - edge, edge), pl.ds(HALO + cols, edge)
    d_both = jnp.concatenate([d_high, d_low], axis=0)
    for copy in load_l:
        copy.wait()
    load_p.wait()
    for at in blocks:
        l_high, l_low = split_bf16(localize[at, :])
        store_panels(high, at, l_high)
        store_panels(low, at, l_low)
        both = dot(d_both, l_high, NT)
        local = both[:stacked] + both[stacked:] + dot(d_high, l_low, NT)
        for c in range(3):
            total = None
            for m in range(members):
                term = perturb[m, c, :, at].astype(jnp.float32) * local[m * cols:(m + 1) * cols]
                total = term if total is None else total + term
            state0[c, own, at] = total
    pl.semaphore_wait(barrier, ens * lon - 1)
    f_copies = [
        remote(state0.at[:, first], state0.at[:, after], left_dev),
        remote(state0.at[:, last], state0.at[:, before], right_dev),
    ]
    for copy in f_copies:
        copy.start()

    load_c.wait()
    states = (state0, state1, state2, state3)
    edge_rows = 2 * 8 * STEPS
    mid_rows = slots_cols - edge_rows

    def keep(n, starts):
        for start in starts:
            value = states[n + 1][0, pl.ds(start, 8), :]
            v_high = value.astype(jnp.bfloat16).astype(jnp.float32)
            if start == HALO or start == HALO + cols - 8:
                row, step = n * 16 + (8 if start > HALO else 0), edge_rows
            else:
                row, step = 2 * edge_rows + n * (cols - 16) + start - HALO - 8, mid_rows
            heights[pl.ds(row, 8), :] = v_high
            heights[pl.ds(row + step, 8), :] = value - v_high

    mid = range(HALO + 8, HALO + cols - 8, 8)
    for n in range(STEPS):
        starts = range(HALO, HALO + cols, 8) if n < STEPS - 1 else mid
        linear_step(states[n], states[n + 1], 1, consts, starts, HALO, HALO + cols)
        keep(n, mid)

    def keys(at):
        cells, slots = cell[:, at], slot[:, at]
        return slots * cols + (cells - cells // cols * cols)

    def scattered(hit, values):
        v_high = values.astype(jnp.bfloat16).astype(jnp.float32)
        return jnp.concatenate(
            [jnp.where(hit, v_high, 0.0), jnp.where(hit, values - v_high, 0.0)], axis=0
        ).astype(jnp.bfloat16)

    def picked(rows_at, at, count, ids_of):
        table = heights[rows_at, :].astype(jnp.bfloat16)
        both = dot(table, panel(onehot, at), NT)
        both = both[:count] + both[count:]
        ids = lax.broadcasted_iota(jnp.int32, both.shape, 0)
        cells, slots = cell[:, at], slot[:, at]
        key = ids_of(slots, cells - cells // cols * cols)
        return jnp.sum(jnp.where(ids == key, both, 0.0), axis=0, keepdims=True)

    def mid_ids(slots, col):
        inside = (col >= 8) & (col < cols - 8)
        return jnp.where(inside, slots * (cols - 16) + col - 8, -1)

    def edge_ids(slots, col):
        place = jnp.where(col < 8, col, col - (cols - 16))
        return jnp.where((col >= 8) & (col < cols - 8), -1, slots * 16 + place)

    def kept(ids_of, count):
        def ids(slots, col):
            key = ids_of(slots, col)
            return jnp.where(slots < STEPS, key, -1)
        return ids

    for at in chunks:
        observed[:, at] = picked(
            pl.ds(2 * edge_rows, 2 * mid_rows), at, mid_rows, kept(mid_ids, mid_rows)
        )

    load_r.wait()
    norm_old = jnp.zeros((8, 128), jnp.float32)
    for at in blocks:
        value = residual[:, :, at]
        norm_old += lane_sum((value * value).reshape(stacked // 8, 8, BLOCK).sum(axis=0))

    for copy in f_copies:
        copy.wait_recv()
    ends = (0, HALO, HALO + cols - 8, HALO + cols)
    for n in range(STEPS):
        linear_step(states[n], states[n + 1], 1, consts, ends, 0, wide)
        keep(n, (HALO, HALO + cols - 8))
    used = pl.ds(0, len(side_rows()))
    peers = [(wrap(me_e + k, ens), me_l) for k in range(1, ens)]
    for k, (n, dist) in enumerate(side_rows()):
        near[0, pl.ds(k, 1), :] = states[n + 1][0, pl.ds(HALO - 1 - n + dist, 1), :]
        near[1, pl.ds(k, 1), :] = states[n + 1][0, pl.ds(HALO + cols + dist, 1), :]
    n_copies = [
        remote(near.at[:, used], near_in.at[j, :, used], peer) for j, peer in enumerate(peers)
    ]

    sums = {}
    for k, at in enumerate(chunks):
        observed[:, at] += picked(pl.ds(0, 2 * edge_rows), at, edge_rows, kept(edge_ids, edge_rows))
        for j, peer in enumerate(peers):
            sums[j, k] = remote(observed.at[:, at], arrived.at[j, :, at], peer)
            sums[j, k].start()
    for copy in n_copies:
        copy.start()

    def side_ids(width):
        row = lax.broadcasted_iota(jnp.int32, (16, 128), 0)
        result = jnp.full((16, 128), -1, jnp.int32)
        for k, (n, dist) in enumerate(side_rows()):
            result = jnp.where(row == k, n * cols + dist, result)
            result = jnp.where(row == 8 + k, n * cols + cols - 1 - n + dist, result)
        return jnp.concatenate([result] * (width // 128), axis=1)

    left = scattered(side_ids(nobs) == keys(pl.ds(0, nobs)), weight[...])
    both = dot(left, panel(onehot, pl.ds(0, nobs)), NN)
    mass[...] = (both[:16] + both[16:]).reshape(2, 8, lat)
    m_copies = [
        remote(mass.at[0, used], mass_in.at[1, used], left_dev),
        remote(mass.at[1, used], mass_in.at[0, used], right_dev),
    ]
    for copy in m_copies:
        copy.start()

    key_ids = lax.broadcasted_iota(jnp.int32, (slots_cols, CHUNK), 0)
    for k, at in enumerate(chunks):
        total = observed[:, at]
        for j in range(ens - 1):
            sums[j, k].wait_recv()
            total = total + arrived[j, :, at]
        left = scattered(key_ids == keys(at), weight[:, at] * total)
        both = dot(left, panel(onehot, at), NN)
        both = both[:slots_cols] + both[slots_cols:]
        if k == 0:
            spread[...] = both
        elif k < len(chunks) - 1:
            spread[...] += both
        else:
            both = spread[...] + both
            for s in range(STEPS):
                forcing[s, own, :] = both[s * cols:(s + 1) * cols]

    for copy in m_copies + n_copies:
        copy.wait_recv()
    for side in range(2):
        total = near[side]
        for j in range(ens - 1):
            total = total + near_in[j, side]
        total = total * mass_in[side]
        for k, (n, dist) in enumerate(side_rows()):
            row = HALO + cols + dist if side else HALO - 1 - n + dist
            forcing[n, pl.ds(row, 1), :] = total[k:k + 1]
    every = range(0, wide, 8)
    inner = range(HALO, HALO + cols, 8)
    linear_step(forcing.at[pl.ds(2, 1)], state1, -1, consts, every, 0, wide, False, forcing.at[1])
    linear_step(state1, state2, -1, consts, every, 0, wide, True, forcing.at[0])
    linear_step(state2, state3, -1, consts, inner, 0, wide)

    for m in range(members):
        total = None
        for c in range(3):
            term = perturb[m, c].astype(jnp.float32) * state3[c, own, :]
            total = term if total is None else total + term
        p_high, p_low = split_bf16(total)
        store_panels(split, pl.ds(m * cols, cols), p_high)
        store_panels(split, pl.ds(stacked + m * cols, cols), p_low)

    p_both = panel(split, pl.ds(0, 2 * stacked))
    sums_new = [norm_old] + [jnp.zeros((8, 128), jnp.float32)] * 3
    for k, at in enumerate(blocks):
        pair = range(k * BLOCK // 128, (k + 1) * BLOCK // 128)
        both = dot(p_both, panel(high, pl.ds(0, lat), pair), NN)
        back = both[:stacked] + both[stacked:]
        back += dot(p_both[:stacked], panel(low, pl.ds(0, lat), pair), NN)
        d = direction[:, :, at].reshape(stacked, BLOCK)
        r = residual[:, :, at].reshape(stacked, BLOCK)
        img = d + back
        image[:, :, at] = img.reshape(members, cols, BLOCK)
        for j, term in enumerate((d * img, r * img, img * img)):
            sums_new[j + 1] += lane_sum(term.reshape(stacked // 8, 8, BLOCK).sum(axis=0))

    tile[...] = pack_rows([jnp.sum(value, axis=0, keepdims=True) for value in sums_new])

    def tell(index, device):
        pltpu.make_async_remote_copy(
            src_ref=tile, dst_ref=tiles.at[index], send_sem=tile_send, recv_sem=tile_recv,
            device_id=device, device_id_type=MESH,
        ).start()

    each_peer(tell)
    load_v.wait()
    for copy in f_copies + m_copies + n_copies + list(sums.values()):
        copy.wait_send()
    everything = pltpu.make_async_remote_copy(
        src_ref=tiles, dst_ref=tiles, send_sem=tile_send, recv_sem=tile_recv,
        device_id=right_dev, device_id_type=MESH,
    )
    everything.wait_send()
    everything.wait_recv()
    norm_old, curvature, cross_term, square = unpack_rows(
        jnp.sum(tiles[...], axis=0) + tile[...], 4
    )
    step_size = norm_old / curvature
    norm_new = norm_old - 2.0 * step_size * cross_term + step_size * step_size * square
    scalars[pl.ds(0, 1), :] = jnp.broadcast_to(step_size, (1, 128))
    scalars[pl.ds(1, 1), :] = jnp.broadcast_to(norm_new / norm_old, (1, 128))


def update(
    control, residual, direction, image, scalars, control_out, residual_out, direction_out,
    control_new, residual_new, direction_new, sem,
):
    step_size, ratio = scalars[pl.ds(0, 1), pl.ds(0, 1)], scalars[pl.ds(1, 1), pl.ds(0, 1)]
    ids = itertools.count()
    copies = []

    def send(src, dst, at):
        copies.append(pltpu.make_async_copy(src.at[at], dst.at[at], sem.at[next(ids)]))
        copies[-1].start()

    members, cols = control.shape[:2]
    for m in range(members):
        for h in range(2):
            at = (m, pl.ds(h * cols // 2, cols // 2))
            d = direction[at]
            new = residual[at] - step_size * image[at]
            residual_new[at] = new
            direction_new[at] = new + ratio * d
            control_new[at] = control[at] + step_size * d
            send(residual_new, residual_out, at)
            send(direction_new, direction_out, at)
            send(control_new, control_out, at)
    for copy in copies:
        copy.wait()


def body(ens, lon, control, residual, direction, ens_perturb, localize, obs_cell, obs_slot, obs_weight):
    flip = functools.partial(jnp.swapaxes, axis1=-1, axis2=-2)
    control, residual, direction, ens_perturb = map(flip, (control, residual, direction, ens_perturb))
    members, cols, lat = direction.shape
    nobs = obs_cell.shape[0]
    count = ens * lon
    wide = cols + 2 * HALO
    f32, bf16, i32 = jnp.float32, jnp.bfloat16, jnp.int32
    hbm = pl.BlockSpec(memory_space=pltpu.HBM)
    dma = pltpu.SemaphoreType.DMA
    field = pltpu.VMEM((members, cols, lat), f32)
    vmem = pl.BlockSpec(memory_space=pltpu.VMEM)
    copies = remote_count(ens, lat, nobs)
    outs = pl.pallas_call(
        functools.partial(kernel, ens, lon),
        out_shape=(field, field, field, field, pltpu.VMEM((8, 128), f32)),
        in_specs=[hbm] * 9,
        out_specs=(vmem,) * 5,
        scratch_shapes=[
            pltpu.VMEM((lat, lat), f32),
            pltpu.VMEM((members, 3, cols, lat), bf16),
            pltpu.VMEM((1, nobs), i32),
            pltpu.VMEM((1, nobs), i32),
            pltpu.VMEM((1, nobs), f32),
            pltpu.VMEM((4, 8, lat), f32),
            pltpu.VMEM((lat // 128, lat, 128), bf16),
            pltpu.VMEM((lat // 128, lat, 128), bf16),
            pltpu.VMEM((lat // 128, 2 * members * cols, 128), bf16),
            pltpu.VMEM((lat // 128, nobs, 128), bf16),
            pltpu.VMEM((3, wide, lat), f32),
            pltpu.VMEM((3, wide, lat), f32),
            pltpu.VMEM((3, wide, lat), f32),
            pltpu.VMEM((3, wide, lat), f32),
            pltpu.VMEM((2 * STEPS * cols, lat), f32),
            pltpu.VMEM((1, nobs), f32),
            pltpu.VMEM((max(ens - 1, 1), 1, nobs), f32),
            pltpu.VMEM((STEPS * cols, lat), f32),
            pltpu.VMEM((STEPS, wide, lat), f32),
            pltpu.VMEM((2, 8, lat), f32),
            pltpu.VMEM((max(ens - 1, 1), 2, 8, lat), f32),
            pltpu.VMEM((2, 8, lat), f32),
            pltpu.VMEM((2, 8, lat), f32),
            pltpu.VMEM((count - 1, 1, 128), f32),
            pltpu.VMEM((1, 128), f32),
            dma((8 + lat // BLOCK,)), dma((copies,)), dma((copies,)),
            dma, dma,
        ],
        compiler_params=pltpu.CompilerParams(
            collective_id=0, has_side_effects=True, vmem_limit_bytes=61 * 1024 * 1024
        ),
    )(
        control, direction, residual, ens_perturb, localize,
        obs_cell.reshape(1, nobs), obs_slot.reshape(1, nobs), obs_weight.reshape(1, nobs),
        jnp.asarray(grid_constants(lat)),
    )
    outs = pl.pallas_call(
        update,
        out_shape=[jax.ShapeDtypeStruct((members, cols, lat), f32)] * 3,
        in_specs=[vmem] * 5,
        out_specs=[hbm] * 3,
        scratch_shapes=[pltpu.VMEM((members, cols, lat), f32)] * 3 + [dma((6 * members,))],
        compiler_params=pltpu.CompilerParams(vmem_limit_bytes=8 * 1024 * 1024),
    )(*outs)
    return tuple(map(flip, outs))


def solution(mesh):
    fields = P("ens", None, "lon")
    in_specs = (fields, fields, fields, P("ens", None, None, "lon"), P(), P("lon"), P("lon"), P("lon"))
    ens, lon = mesh.shape["ens"], mesh.shape["lon"]
    return jax.shard_map(
        functools.partial(body, ens, lon), mesh=mesh, in_specs=in_specs,
        out_specs=(fields, fields, fields), check_vma=False,
    )
```

time: 39.2 us -> 28.9 us (0.74)
  Pallas kernels: 34.6 us -> 28 us
  other arithmetic: 3.7 us -> 0 us
    pallas_call x1 -> x2, Pallas kernels: 34.6 us -> 28 us  [the longest x1 26.7 us: body(): pl.pallas_call(functools.partial(kernel, ens, lon), out_shape=(field, fie...]
    transpose x1 -> x0, other arithmetic: 2.17 us -> none  [body(): return tuple(map(flip, (control_new, residual_new, direction_new)))]
    add x1 -> x0, other arithmetic: 1.54 us -> none  [body(): control_new = control + step_size * direction]
where the time goes in v2:
time: 28.9 us; the launch traced here: 28.6 us
  Pallas kernels  28 us (97%)
  between operations  0.64 us (2%)
    pallas_call x1, Pallas kernels, body(): pl.pallas_call(functools.partial(kernel, ens, lon), out_shape=(field, fie...  26.7 us
    pallas_call x1, Pallas kernels, body(): pl.pallas_call(update, out_shape=[jax.ShapeDtypeStruct((members, cols, la...  1.29 us

profile of v2, /device:TPU:0, one launch (start us, length us, event | category | flops | bytes accessed | tf_op | source)
XLA Modules:
  0.0 28.6 jit_solution(3160323529585499203)
XLA Ops:
  0.6 26.7 %shard_map.112 = (f32[2,64,1024]{2,1,0:T(8,128)S(1)}, f32[2,64,1024]{2,1,0:T(8,128)S(1)}, f32[2,64,1024]{2,1,0:T(8,128)S(1)}, f32[2,64,1024]{2,1,0:T(8,128)S(1)}, f32[8,128]{1,0:T(8,128)S(1)}) custom-call(f32[2,64,1024]{2,1,0:T(8,128)} %bitcast.11, f32[2,64,1024]{2,1,0:T(8,128)} %bitcast.12, f32[2,64,1024]{2,1,0:T(8,128)} %bitcast.13, ...), custom_call_target="tpu_custom_call" | custom-call | tf_op jit(solution)/shard_map/pallas_call | solution.py:463
  27.3 1.3 %shard_map.113 = (f32[2,64,1024]{2,1,0:T(8,128)}, f32[2,64,1024]{2,1,0:T(8,128)}, f32[2,64,1024]{2,1,0:T(8,128)}) custom-call(f32[2,64,1024]{2,1,0:T(8,128)S(1)} %get-tuple-element.11.control, f32[2,64,1024]{2,1,0:T(8,128)S(1)} %get-tuple-element.12.residual, f32[2,64,1024]{2,1,0:T(8,128)S(1)} %get-tuple-element.13.direction, ...), custom_call_target="tpu_custom_call" | custom-call | tf_op jit(solution)/shard_map/pallas_call | solution.py:505

commit v3 on v2

--- a/solution.py
+++ b/solution.py
@@ -11,7 +11,8 @@
 
 STEPS = 3
 HALO = 8
-CHUNK = 2048
+HALF = 0.5 * 0.35
+SHARES = (0, 2, 4, 6, 8)
 BLOCK = 256
 MESH = pl.DeviceIdType.MESH
 NT = (((1,), (1,)), ((), ()))
@@ -30,18 +31,14 @@
 
 def grid_constants(lat):
     phi = np.pi * (-1.0 / 3.0 + 2.0 / 3.0 * (np.arange(lat) + 0.5) / lat)
-    half = 0.5 * 0.35
-    up = np.full(lat, half)
-    up[-1] = 0.0
-    down = np.full(lat, half)
-    down[0] = 0.0
-    rows = np.stack([half / np.cos(phi), 0.2 * np.sin(phi), up, down])
-    return np.ascontiguousarray(np.broadcast_to(rows[:, None], (4, 8, lat))).astype(np.float32)
+    rows = np.stack([HALF / np.cos(phi), 0.2 * np.sin(phi)])
+    return np.ascontiguousarray(np.broadcast_to(rows[:, None], (2, 8, lat))).astype(np.float32)
 
 
 def linear_step(source, target, sign, consts, blocks, low_end, high_end, rest=True, extra=None):
     lat = source.shape[2]
-    lon_c, cor_c, up_c, down_c = (consts[k] for k in range(4))
+    lon_c, cor_c = consts[0], consts[1]
+    lane = lax.broadcasted_iota(jnp.int32, (8, 128), 1)
 
     def less(value, term):
         return value - term if sign > 0 else value + term
@@ -61,7 +58,12 @@
             return lon_c * (east - west)
 
         def lat_diff(block):
-            return up_c * pltpu.roll(block, lat - 1, 1) - down_c * pltpu.roll(block, 1, 1)
+            up, down = pltpu.roll(block, lat - 1, 1), pltpu.roll(block, 1, 1)
+            up_end = jnp.where(lane == 127, 0.0, up[:, lat - 128:])
+            down_end = jnp.where(lane == 0, 0.0, down[:, :128])
+            up = jnp.concatenate([up[:, :lat - 128], up_end], axis=1)
+            down = jnp.concatenate([down_end, down[:, 128:]], axis=1)
+            return HALF * (up - down)
 
         height = source[0, here, :]
         along_lon, along_lat = lon_diff(0, height), lat_diff(height)
@@ -105,7 +107,7 @@
 
 
 def remote_count(ens, lat, nobs):
-    return 4 + (ens - 1) * (1 + nobs // CHUNK)
+    return 4 + (ens - 1) * len(SHARES)
 
 
 def side_rows():
@@ -128,7 +130,8 @@
     stacked = members * cols
     slots_cols = STEPS * cols
     blocks = [pl.ds(k, BLOCK) for k in range(0, lat, BLOCK)]
-    chunks = [pl.ds(k, CHUNK) for k in range(0, nobs, CHUNK)]
+    cuts = [nobs * share // SHARES[-1] for share in SHARES]
+    chunks = [pl.ds(start, stop - start) for start, stop in zip(cuts, cuts[1:])]
     panels = range(lat // 128)
 
     def wrap(value, size):
@@ -146,8 +149,9 @@
 
     load_obs = [load(cell_hbm, cell), load(slot_hbm, slot), load(weight_hbm, weight)]
     load_d = load(direction_hbm, direction)
-    load_l = [load(localize_hbm.at[at, :], localize.at[at, :]) for at in blocks]
+    load_l = [load(localize_hbm.at[at, :], localize.at[at, :]) for at in blocks[:2]]
     load_p = load(perturb_hbm, perturb)
+    load_l += [load(localize_hbm.at[at, :], localize.at[at, :]) for at in blocks[2:]]
     load_c = load(consts_hbm, consts)
     load_r = load(residual_hbm, residual)
     load_v = load(control_hbm, control)
@@ -182,12 +186,18 @@
     rows = jnp.concatenate([rows] * (128 * 128 // nobs), axis=0).T
     lanes = lax.broadcasted_iota(jnp.int32, (16, 128), 1).astype(jnp.int16)
     one, zero = jnp.ones((16, 128), jnp.bfloat16), jnp.zeros((16, 128), jnp.bfloat16)
-    for group in range(nobs // 128):
-        for s in range(0, 128, 16):
-            row = jnp.broadcast_to(rows[s:s + 16, group:group + 1], (16, 128)).astype(jnp.int16)
-            for j in panels:
-                hit = row == lanes + jnp.int16(128 * j)
-                onehot[j, pl.ds(128 * group + s, 16), :] = jnp.where(hit, one, zero)
+
+    def mark(groups):
+        for group in groups:
+            for s in range(0, 128, 16):
+                row = jnp.broadcast_to(rows[s:s + 16, group:group + 1], (16, 128))
+                row = row.astype(jnp.int16)
+                for j in panels:
+                    hit = row == lanes + jnp.int16(128 * j)
+                    onehot[j, pl.ds(128 * group + s, 16), :] = jnp.where(hit, one, zero)
+
+    groups = nobs // 128
+    mark(range(0, groups // 2))
 
     def panel(ref, at, which=panels):
         return jnp.concatenate([ref[j, at, :] for j in which], axis=1)
@@ -204,10 +214,13 @@
     first, last = pl.ds(HALO, edge), pl.ds(HALO + cols - edge, edge)
     before, after = pl.ds(HALO - edge, edge), pl.ds(HALO + cols, edge)
     d_both = jnp.concatenate([d_high, d_low], axis=0)
-    for copy in load_l:
-        copy.wait()
-    load_p.wait()
-    for at in blocks:
+    mark(range(groups // 2, groups * 3 // 4))
+    for k, at in enumerate(blocks):
+        if k % 2 == 0:
+            load_l[k].wait()
+            load_l[k + 1].wait()
+            if k == 0:
+                load_p.wait()
         l_high, l_low = split_bf16(localize[at, :])
         store_panels(high, at, l_high)
         store_panels(low, at, l_low)
@@ -219,6 +232,52 @@
                 term = perturb[m, c, :, at].astype(jnp.float32) * local[m * cols:(m + 1) * cols]
                 total = term if total is None else total + term
             state0[c, own, at] = total
+        mark(range(groups * (12 + k) // 16, groups * (13 + k) // 16))
+    def keys(at):
+        cells, slots = cell[:, at], slot[:, at]
+        return slots * cols + (cells - cells // cols * cols)
+
+    def scattered(hit, values):
+        v_high = values.astype(jnp.bfloat16).astype(jnp.float32)
+        return jnp.concatenate(
+            [jnp.where(hit, v_high, 0.0), jnp.where(hit, values - v_high, 0.0)], axis=0
+        ).astype(jnp.bfloat16)
+
+    load_c.wait()
+    load_r.wait()
+    states = (state0, state1, state2, state3)
+
+    def keep(n, starts):
+        for start in starts:
+            value = states[n + 1][0, pl.ds(start, 8), :]
+            v_high = value.astype(jnp.bfloat16).astype(jnp.float32)
+            row = n * cols + start - HALO
+            heights[pl.ds(row, 8), :] = v_high
+            heights[pl.ds(slots_cols + row, 8), :] = value - v_high
+
+    mid = range(HALO + 8, HALO + cols - 8, 8)
+    def side_ids(width):
+        row = lax.broadcasted_iota(jnp.int32, (16, 128), 0)
+        result = jnp.full((16, 128), -1, jnp.int32)
+        for k, (n, dist) in enumerate(side_rows()):
+            result = jnp.where(row == k, n * cols + dist, result)
+            result = jnp.where(row == 8 + k, n * cols + cols - 1 - n + dist, result)
+        return jnp.concatenate([result] * (width // 128), axis=1)
+
+
+    def before_halo():
+        for n in range(STEPS):
+            starts = range(HALO, HALO + cols, 8) if n < STEPS - 1 else mid
+            linear_step(states[n], states[n + 1], 1, consts, starts, HALO, HALO + cols)
+            keep(n, mid)
+
+        left = scattered(side_ids(nobs) == keys(pl.ds(0, nobs)), weight[...])
+        both = dot(left, panel(onehot, pl.ds(0, nobs)), NN)
+        mass[...] = (both[:16] + both[16:]).reshape(2, 8, lat)
+
+    is_first = (me_l == 0) & (me_e == 0)
+    pl.when(is_first)(before_halo)
+
     pl.semaphore_wait(barrier, ens * lon - 1)
     f_copies = [
         remote(state0.at[:, first], state0.at[:, after], left_dev),
@@ -227,71 +286,63 @@
     for copy in f_copies:
         copy.start()
 
-    load_c.wait()
-    states = (state0, state1, state2, state3)
-    edge_rows = 2 * 8 * STEPS
-    mid_rows = slots_cols - edge_rows
-
-    def keep(n, starts):
-        for start in starts:
-            value = states[n + 1][0, pl.ds(start, 8), :]
-            v_high = value.astype(jnp.bfloat16).astype(jnp.float32)
-            if start == HALO or start == HALO + cols - 8:
-                row, step = n * 16 + (8 if start > HALO else 0), edge_rows
-            else:
-                row, step = 2 * edge_rows + n * (cols - 16) + start - HALO - 8, mid_rows
-            heights[pl.ds(row, 8), :] = v_high
-            heights[pl.ds(row + step, 8), :] = value - v_high
-
-    mid = range(HALO + 8, HALO + cols - 8, 8)
-    for n in range(STEPS):
-        starts = range(HALO, HALO + cols, 8) if n < STEPS - 1 else mid
-        linear_step(states[n], states[n + 1], 1, consts, starts, HALO, HALO + cols)
-        keep(n, mid)
-
-    def keys(at):
-        cells, slots = cell[:, at], slot[:, at]
-        return slots * cols + (cells - cells // cols * cols)
-
-    def scattered(hit, values):
-        v_high = values.astype(jnp.bfloat16).astype(jnp.float32)
-        return jnp.concatenate(
-            [jnp.where(hit, v_high, 0.0), jnp.where(hit, values - v_high, 0.0)], axis=0
-        ).astype(jnp.bfloat16)
-
-    def picked(rows_at, at, count, ids_of):
-        table = heights[rows_at, :].astype(jnp.bfloat16)
-        both = dot(table, panel(onehot, at), NT)
-        both = both[:count] + both[count:]
-        ids = lax.broadcasted_iota(jnp.int32, both.shape, 0)
-        cells, slots = cell[:, at], slot[:, at]
-        key = ids_of(slots, cells - cells // cols * cols)
-        return jnp.sum(jnp.where(ids == key, both, 0.0), axis=0, keepdims=True)
-
-    def mid_ids(slots, col):
-        inside = (col >= 8) & (col < cols - 8)
-        return jnp.where(inside, slots * (cols - 16) + col - 8, -1)
-
-    def edge_ids(slots, col):
-        place = jnp.where(col < 8, col, col - (cols - 16))
-        return jnp.where((col >= 8) & (col < cols - 8), -1, slots * 16 + place)
-
-    def kept(ids_of, count):
-        def ids(slots, col):
-            key = ids_of(slots, col)
-            return jnp.where(slots < STEPS, key, -1)
-        return ids
-
-    for at in chunks:
-        observed[:, at] = picked(
-            pl.ds(2 * edge_rows, 2 * mid_rows), at, mid_rows, kept(mid_ids, mid_rows)
-        )
-
-    load_r.wait()
+    pl.when(jnp.logical_not(is_first))(before_halo)
     norm_old = jnp.zeros((8, 128), jnp.float32)
     for at in blocks:
         value = residual[:, :, at]
         norm_old += lane_sum((value * value).reshape(stacked // 8, 8, BLOCK).sum(axis=0))
+
+    used = pl.ds(0, len(side_rows()))
+    m_copies = [
+        remote(mass.at[0, used], mass_in.at[1, used], left_dev),
+        remote(mass.at[1, used], mass_in.at[0, used], right_dev),
+    ]
+    for copy in m_copies:
+        copy.start()
+
+    is_end = me_l == 0
+    mid_cols = cols - 16
+    key_ids = lax.broadcasted_iota(jnp.int32, (slots_cols, nobs), 0)
+
+    def gather(ranges, key_of, done):
+        rows = [
+            pl.ds(h * slots_cols + n * cols + start, size)
+            for h in range(2) for n in range(STEPS) for start, size in ranges
+        ]
+        table = jnp.concatenate([heights[row, :] for row in rows], axis=0).astype(jnp.bfloat16)
+        count = table.shape[0] // 2
+
+        def finish(k, both):
+            at = chunks[k]
+            slots, key = slot[:, at], keys(at)
+            key = key_of(slots, key - slots * cols)
+            both = both[:count] + both[count:]
+            both = jnp.where(key_ids[:count, :both.shape[1]] == key, both, 0.0)
+            done(k, at, jnp.sum(both, axis=0, keepdims=True))
+
+        ahead = None
+        for k, at in enumerate(chunks):
+            both = dot(table, panel(onehot, at), NT)
+            if ahead is not None:
+                finish(k - 1, ahead)
+            ahead = both
+        finish(len(chunks) - 1, ahead)
+
+    def mid_key(slots, col):
+        inside = (col >= 8) & (col < cols - 8) & (slots < STEPS)
+        return jnp.where(inside, slots * mid_cols + col - 8, -1)
+
+    def edge_key(slots, col):
+        inside = (col >= 8) & (col < cols - 8)
+        place = jnp.where(col < 8, col, col - mid_cols)
+        return jnp.where(inside | (slots >= STEPS), -1, slots * 16 + place)
+
+    @pl.when(is_end)
+    def _():
+        def done(k, at, values):
+            observed[:, at] = values
+
+        gather([(8, mid_cols)], mid_key, done)
 
     for copy in f_copies:
         copy.wait_recv()
@@ -299,8 +350,16 @@
     for n in range(STEPS):
         linear_step(states[n], states[n + 1], 1, consts, ends, 0, wide)
         keep(n, (HALO, HALO + cols - 8))
-    used = pl.ds(0, len(side_rows()))
-    peers = [(wrap(me_e + k, ens), me_l) for k in range(1, ens)]
+    tall = 2 if ens % 2 == 0 else 1
+    broad = ens // tall
+    me_a = me_e // broad
+    me_b = me_e - me_a * broad
+    straight = [(0, j) for j in range(1, broad)] + [(i, 0) for i in range(1, tall)]
+    slanted = [(i, j) for i in range(1, tall) for j in range(1, broad)]
+    peers = [
+        (wrap(me_a + i, tall) * broad + wrap(me_b + j, broad), me_l)
+        for i, j in straight + slanted
+    ]
     for k, (n, dist) in enumerate(side_rows()):
         near[0, pl.ds(k, 1), :] = states[n + 1][0, pl.ds(HALO - 1 - n + dist, 1), :]
         near[1, pl.ds(k, 1), :] = states[n + 1][0, pl.ds(HALO + cols + dist, 1), :]
@@ -308,40 +367,44 @@
         remote(near.at[:, used], near_in.at[j, :, used], peer) for j, peer in enumerate(peers)
     ]
 
-    sums = {}
+    for copy in n_copies[:len(straight)]:
+        copy.start()
+
+    sums = {
+        (j, k): remote(observed.at[:, at], arrived.at[j, :, at], peer)
+        for k, at in enumerate(chunks) for j, peer in enumerate(peers)
+    }
+
+    def send(k):
+        for j in range(ens - 1):
+            sums[j, k].start()
+        if k == 0:
+            for copy in n_copies[len(straight):]:
+                copy.start()
+
+    @pl.when(is_end)
+    def _():
+        def done(k, at, values):
+            observed[:, at] += values
+            send(k)
+
+        gather([(0, 8), (cols - 8, 8)], edge_key, done)
+
+    @pl.when(jnp.logical_not(is_end))
+    def _():
+        def done(k, at, values):
+            observed[:, at] = values
+            send(k)
+
+        gather([(0, cols)], lambda slots, col: slots * cols + col, done)
+
     for k, at in enumerate(chunks):
-        observed[:, at] += picked(pl.ds(0, 2 * edge_rows), at, edge_rows, kept(edge_ids, edge_rows))
-        for j, peer in enumerate(peers):
-            sums[j, k] = remote(observed.at[:, at], arrived.at[j, :, at], peer)
-            sums[j, k].start()
-    for copy in n_copies:
-        copy.start()
-
-    def side_ids(width):
-        row = lax.broadcasted_iota(jnp.int32, (16, 128), 0)
-        result = jnp.full((16, 128), -1, jnp.int32)
-        for k, (n, dist) in enumerate(side_rows()):
-            result = jnp.where(row == k, n * cols + dist, result)
-            result = jnp.where(row == 8 + k, n * cols + cols - 1 - n + dist, result)
-        return jnp.concatenate([result] * (width // 128), axis=1)
-
-    left = scattered(side_ids(nobs) == keys(pl.ds(0, nobs)), weight[...])
-    both = dot(left, panel(onehot, pl.ds(0, nobs)), NN)
-    mass[...] = (both[:16] + both[16:]).reshape(2, 8, lat)
-    m_copies = [
-        remote(mass.at[0, used], mass_in.at[1, used], left_dev),
-        remote(mass.at[1, used], mass_in.at[0, used], right_dev),
-    ]
-    for copy in m_copies:
-        copy.start()
-
-    key_ids = lax.broadcasted_iota(jnp.int32, (slots_cols, CHUNK), 0)
-    for k, at in enumerate(chunks):
+        for j in range(ens - 1):
+            sums[j, k].wait_recv()
         total = observed[:, at]
         for j in range(ens - 1):
-            sums[j, k].wait_recv()
             total = total + arrived[j, :, at]
-        left = scattered(key_ids == keys(at), weight[:, at] * total)
+        left = scattered(key_ids[:, :total.shape[1]] == keys(at), weight[:, at] * total)
         both = dot(left, panel(onehot, at), NN)
         both = both[:slots_cols] + both[slots_cols:]
         if k == 0:
@@ -471,7 +534,7 @@
             pltpu.VMEM((1, nobs), i32),
             pltpu.VMEM((1, nobs), i32),
             pltpu.VMEM((1, nobs), f32),
-            pltpu.VMEM((4, 8, lat), f32),
+            pltpu.VMEM((2, 8, lat), f32),
             pltpu.VMEM((lat // 128, lat, 128), bf16),
             pltpu.VMEM((lat // 128, lat, 128), bf16),
             pltpu.VMEM((lat // 128, 2 * members * cols, 128), bf16),

time: 28.9 us -> 28.3 us (0.979)
  Pallas kernels: 28 us -> 27.2 us
    pallas_call x1, Pallas kernels: 26.7 us -> 26 us  [body(): pl.pallas_call(functools.partial(kernel, ens, lon), out_shape=(field, fie...]
where the time goes in v3:
time: 28.3 us; the launch traced here: 28 us
  Pallas kernels  27.2 us (96%)
  between operations  0.8 us (3%)
    pallas_call x1, Pallas kernels, body(): pl.pallas_call(functools.partial(kernel, ens, lon), out_shape=(field, fie...  26 us
    pallas_call x1, Pallas kernels, body(): pl.pallas_call(update, out_shape=[jax.ShapeDtypeStruct((members, cols, la...  1.29 us

profile of v3, /device:TPU:0, one launch (start us, length us, event | category | flops | bytes accessed | tf_op | source)
XLA Modules:
  0.0 28.0 jit_solution(2533728224338517627)
XLA Ops:
  0.6 26.0 %shard_map.112 = (f32[2,64,1024]{2,1,0:T(8,128)S(1)}, f32[2,64,1024]{2,1,0:T(8,128)S(1)}, f32[2,64,1024]{2,1,0:T(8,128)S(1)}, f32[2,64,1024]{2,1,0:T(8,128)S(1)}, f32[8,128]{1,0:T(8,128)S(1)}) custom-call(f32[2,64,1024]{2,1,0:T(8,128)} %bitcast.11, f32[2,64,1024]{2,1,0:T(8,128)} %bitcast.12, f32[2,64,1024]{2,1,0:T(8,128)} %bitcast.13, ...), custom_call_target="tpu_custom_call" | custom-call | tf_op jit(solution)/shard_map/pallas_call | solution.py:526
  26.6 1.3 %shard_map.113 = (f32[2,64,1024]{2,1,0:T(8,128)}, f32[2,64,1024]{2,1,0:T(8,128)}, f32[2,64,1024]{2,1,0:T(8,128)}) custom-call(f32[2,64,1024]{2,1,0:T(8,128)S(1)} %get-tuple-element.11.control, f32[2,64,1024]{2,1,0:T(8,128)S(1)} %get-tuple-element.12.residual, f32[2,64,1024]{2,1,0:T(8,128)S(1)} %get-tuple-element.13.direction, ...), custom_call_target="tpu_custom_call" | custom-call | tf_op jit(solution)/shard_map/pallas_call | solution.py:568

commit v4 on v3

--- a/solution.py
+++ b/solution.py
@@ -12,7 +12,7 @@
 STEPS = 3
 HALO = 8
 HALF = 0.5 * 0.35
-SHARES = (0, 2, 4, 6, 8)
+SHARES = (0, 4, 8, 13, 16)
 BLOCK = 256
 MESH = pl.DeviceIdType.MESH
 NT = (((1,), (1,)), ((), ()))
@@ -106,8 +106,7 @@
     return total
 
 
-def remote_count(ens, lat, nobs):
-    return 4 + (ens - 1) * len(SHARES)
+LEFT_COPY, RIGHT_COPY, MASS_COPY, NEAR_COPY, LATE_COPY, SUM_COPY = range(6)
 
 
 def side_rows():
@@ -149,32 +148,34 @@
 
     load_obs = [load(cell_hbm, cell), load(slot_hbm, slot), load(weight_hbm, weight)]
     load_d = load(direction_hbm, direction)
-    load_l = [load(localize_hbm.at[at, :], localize.at[at, :]) for at in blocks[:2]]
+    halves = [pl.ds(k, lat // 2) for k in (0, lat // 2)]
+    load_l = [load(localize_hbm.at[halves[0]], localize.at[halves[0]])]
     load_p = load(perturb_hbm, perturb)
-    load_l += [load(localize_hbm.at[at, :], localize.at[at, :]) for at in blocks[2:]]
+    load_l.append(load(localize_hbm.at[halves[1]], localize.at[halves[1]]))
     load_c = load(consts_hbm, consts)
     load_r = load(residual_hbm, residual)
     load_v = load(control_hbm, control)
 
     barrier = pltpu.get_barrier_semaphore()
-    ids = itertools.count()
-
-    def remote(src, dst, device):
-        k = next(ids)
+
+    def remote(src, dst, device, kind, arrival):
         return pltpu.make_async_remote_copy(
-            src_ref=src, dst_ref=dst, send_sem=send_sem.at[k], recv_sem=recv_sem.at[k],
+            src_ref=src, dst_ref=dst, send_sem=send_sem.at[kind], recv_sem=recv_sem.at[arrival],
             device_id=device, device_id_type=MESH,
         )
 
+    def all_of(ref, kind, arrival):
+        return remote(ref, ref, right_dev, kind, arrival)
+
+    order = sorted(range(lon), key=lambda l: (l == 0, min(l, lon - l), l))
+
     def each_peer(act):
-        for e in range(ens):
-            peer_e = wrap(me_e + e, ens)
-
-            def visit(l, carry):
-                act(e * lon + l - 1, (peer_e, wrap(me_l + l, lon)))
-                return carry
-
-            lax.fori_loop(0 if e else 1, lon, visit, 0, unroll=True)
+        peers_e = [wrap(me_e + e, ens) for e in range(ens)]
+        for l in order:
+            peer_l = wrap(me_l + l, lon)
+            for e in range(ens):
+                if e or l:
+                    act(e * lon + l - 1, (peers_e[e], peer_l))
 
     each_peer(lambda index, device: pl.semaphore_signal(
         barrier, inc=1, device_id=device, device_id_type=MESH
@@ -216,9 +217,8 @@
     d_both = jnp.concatenate([d_high, d_low], axis=0)
     mark(range(groups // 2, groups * 3 // 4))
     for k, at in enumerate(blocks):
-        if k % 2 == 0:
-            load_l[k].wait()
-            load_l[k + 1].wait()
+        if k % (len(blocks) // 2) == 0:
+            load_l[k // (len(blocks) // 2)].wait()
             if k == 0:
                 load_p.wait()
         l_high, l_low = split_bf16(localize[at, :])
@@ -255,7 +255,7 @@
             heights[pl.ds(row, 8), :] = v_high
             heights[pl.ds(slots_cols + row, 8), :] = value - v_high
 
-    mid = range(HALO + 8, HALO + cols - 8, 8)
+    inner = range(HALO, HALO + cols, 8)
     def side_ids(width):
         row = lax.broadcasted_iota(jnp.int32, (16, 128), 0)
         result = jnp.full((16, 128), -1, jnp.int32)
@@ -267,9 +267,8 @@
 
     def before_halo():
         for n in range(STEPS):
-            starts = range(HALO, HALO + cols, 8) if n < STEPS - 1 else mid
-            linear_step(states[n], states[n + 1], 1, consts, starts, HALO, HALO + cols)
-            keep(n, mid)
+            linear_step(states[n], states[n + 1], 1, consts, inner, HALO, HALO + cols)
+            keep(n, inner)
 
         left = scattered(side_ids(nobs) == keys(pl.ds(0, nobs)), weight[...])
         both = dot(left, panel(onehot, pl.ds(0, nobs)), NN)
@@ -280,8 +279,8 @@
 
     pl.semaphore_wait(barrier, ens * lon - 1)
     f_copies = [
-        remote(state0.at[:, first], state0.at[:, after], left_dev),
-        remote(state0.at[:, last], state0.at[:, before], right_dev),
+        remote(state0.at[:, first], state0.at[:, after], left_dev, LEFT_COPY, 0),
+        remote(state0.at[:, last], state0.at[:, before], right_dev, RIGHT_COPY, 1),
     ]
     for copy in f_copies:
         copy.start()
@@ -294,62 +293,15 @@
 
     used = pl.ds(0, len(side_rows()))
     m_copies = [
-        remote(mass.at[0, used], mass_in.at[1, used], left_dev),
-        remote(mass.at[1, used], mass_in.at[0, used], right_dev),
+        remote(mass.at[0, used], mass_in.at[1, used], left_dev, MASS_COPY, 2),
+        remote(mass.at[1, used], mass_in.at[0, used], right_dev, MASS_COPY, 2),
     ]
     for copy in m_copies:
         copy.start()
 
-    is_end = me_l == 0
-    mid_cols = cols - 16
+    is_left, is_right = me_l == 0, me_l == lon - 1
+    is_end = is_left | is_right
     key_ids = lax.broadcasted_iota(jnp.int32, (slots_cols, nobs), 0)
-
-    def gather(ranges, key_of, done):
-        rows = [
-            pl.ds(h * slots_cols + n * cols + start, size)
-            for h in range(2) for n in range(STEPS) for start, size in ranges
-        ]
-        table = jnp.concatenate([heights[row, :] for row in rows], axis=0).astype(jnp.bfloat16)
-        count = table.shape[0] // 2
-
-        def finish(k, both):
-            at = chunks[k]
-            slots, key = slot[:, at], keys(at)
-            key = key_of(slots, key - slots * cols)
-            both = both[:count] + both[count:]
-            both = jnp.where(key_ids[:count, :both.shape[1]] == key, both, 0.0)
-            done(k, at, jnp.sum(both, axis=0, keepdims=True))
-
-        ahead = None
-        for k, at in enumerate(chunks):
-            both = dot(table, panel(onehot, at), NT)
-            if ahead is not None:
-                finish(k - 1, ahead)
-            ahead = both
-        finish(len(chunks) - 1, ahead)
-
-    def mid_key(slots, col):
-        inside = (col >= 8) & (col < cols - 8) & (slots < STEPS)
-        return jnp.where(inside, slots * mid_cols + col - 8, -1)
-
-    def edge_key(slots, col):
-        inside = (col >= 8) & (col < cols - 8)
-        place = jnp.where(col < 8, col, col - mid_cols)
-        return jnp.where(inside | (slots >= STEPS), -1, slots * 16 + place)
-
-    @pl.when(is_end)
-    def _():
-        def done(k, at, values):
-            observed[:, at] = values
-
-        gather([(8, mid_cols)], mid_key, done)
-
-    for copy in f_copies:
-        copy.wait_recv()
-    ends = (0, HALO, HALO + cols - 8, HALO + cols)
-    for n in range(STEPS):
-        linear_step(states[n], states[n + 1], 1, consts, ends, 0, wide)
-        keep(n, (HALO, HALO + cols - 8))
     tall = 2 if ens % 2 == 0 else 1
     broad = ens // tall
     me_a = me_e // broad
@@ -360,47 +312,101 @@
         (wrap(me_a + i, tall) * broad + wrap(me_b + j, broad), me_l)
         for i, j in straight + slanted
     ]
-    for k, (n, dist) in enumerate(side_rows()):
-        near[0, pl.ds(k, 1), :] = states[n + 1][0, pl.ds(HALO - 1 - n + dist, 1), :]
-        near[1, pl.ds(k, 1), :] = states[n + 1][0, pl.ds(HALO + cols + dist, 1), :]
     n_copies = [
-        remote(near.at[:, used], near_in.at[j, :, used], peer) for j, peer in enumerate(peers)
+        [
+            remote(near.at[part, used], near_in.at[j, part, used], peer, kind, arrival)
+            for part, kind, arrival in ((0, NEAR_COPY, 3), (1, NEAR_COPY, 3), (2, LATE_COPY, 4))
+        ]
+        for j, peer in enumerate(peers)
     ]
-
-    for copy in n_copies[:len(straight)]:
-        copy.start()
-
     sums = {
-        (j, k): remote(observed.at[:, at], arrived.at[j, :, at], peer)
+        (j, k): remote(observed.at[:, at], arrived.at[j, :, at], peer, SUM_COPY, 5 + k)
         for k, at in enumerate(chunks) for j, peer in enumerate(peers)
     }
-
-    def send(k):
-        for j in range(ens - 1):
-            sums[j, k].start()
-        if k == 0:
-            for copy in n_copies[len(straight):]:
-                copy.start()
+    far = (is_left, is_right)
+    own_edge = (
+        lambda n, dist: HALO + dist,
+        lambda n, dist: HALO + cols - 1 - n + dist,
+    )
+    beyond = (
+        lambda n, dist: HALO - 1 - n + dist,
+        lambda n, dist: HALO + cols + dist,
+    )
+
+    def outer(side):
+        starts = (HALO + cols - 8, HALO + cols) if side else (0, HALO)
+        f_copies[1 - side].wait_recv()
+        for n in range(STEPS):
+            linear_step(states[n], states[n + 1], 1, consts, starts, 0, wide)
+            keep(n, starts[:1] if side else starts[1:])
+        for k, (n, dist) in enumerate(side_rows()):
+            near[side, pl.ds(k, 1), :] = states[n + 1][0, pl.ds(beyond[side](n, dist), 1), :]
+
+    def outer_late(side):
+        outer(side)
+        for k, (n, dist) in enumerate(side_rows()):
+            near[2, pl.ds(k, 1), :] = states[n + 1][0, pl.ds(own_edge[side](n, dist), 1), :]
+        for parts in n_copies:
+            parts[side].start()
+            parts[2].start()
+
+    for side in range(2):
+        @pl.when(jnp.logical_not(far[side]))
+        def _():
+            outer(side)
+            for parts in n_copies[:len(straight)]:
+                parts[side].start()
+
+    first_own = jnp.where(is_left, 0, -cols)
+    last_own = jnp.where(is_right, cols - 1, 2 * cols)
+
+    def gather(which, after_first):
+        table = heights[...].astype(jnp.bfloat16)
+
+        def finish(k, both):
+            at = chunks[k]
+            slots, key = slot[:, at], keys(at)
+            col = key - slots * cols
+            late = (col <= slots + first_own) | (col >= last_own - slots)
+            both = both[:slots_cols] + both[slots_cols:]
+            hit = key_ids[:, :both.shape[1]] == jnp.where(late, -1, key)
+            observed[:, at] = jnp.sum(jnp.where(hit, both, 0.0), axis=0, keepdims=True)
+            for j in range(ens - 1):
+                sums[j, k].start()
+            if k == 0:
+                after_first()
+
+        ahead = None
+        for k in which:
+            both = dot(table, panel(onehot, chunks[k]), NT)
+            if ahead is not None:
+                finish(*ahead)
+            ahead = (k, both)
+        finish(*ahead)
+
+    number = len(chunks)
+
+    def slanted_start(sides):
+        for parts in n_copies[len(straight):]:
+            for side in sides:
+                parts[side].start()
 
     @pl.when(is_end)
     def _():
-        def done(k, at, values):
-            observed[:, at] += values
-            send(k)
-
-        gather([(0, 8), (cols - 8, 8)], edge_key, done)
+        gather(range(number - 1), lambda: None)
+        for side in range(2):
+            @pl.when(far[side])
+            def _():
+                slanted_start((1 - side,))
+                outer_late(side)
+        gather(range(number - 1, number), lambda: None)
 
     @pl.when(jnp.logical_not(is_end))
     def _():
-        def done(k, at, values):
-            observed[:, at] = values
-            send(k)
-
-        gather([(0, cols)], lambda slots, col: slots * cols + col, done)
+        gather(range(number), lambda: slanted_start(range(2)))
 
     for k, at in enumerate(chunks):
-        for j in range(ens - 1):
-            sums[j, k].wait_recv()
+        all_of(arrived.at[:, :, at], SUM_COPY, 5 + k).wait_recv()
         total = observed[:, at]
         for j in range(ens - 1):
             total = total + arrived[j, :, at]
@@ -416,18 +422,31 @@
             for s in range(STEPS):
                 forcing[s, own, :] = both[s * cols:(s + 1) * cols]
 
-    for copy in m_copies + n_copies:
-        copy.wait_recv()
+    both_sides = pl.ds(0, 2)
+    m_all = all_of(mass_in.at[:, used], MASS_COPY, 2)
+    n_all = all_of(near_in.at[:, both_sides, used], NEAR_COPY, 3)
+    late_all = all_of(near_in.at[:, 2, used], LATE_COPY, 4)
+    m_all.wait_recv()
+    n_all.wait_recv()
+
+    def summed(part):
+        total = near[part]
+        for j in range(ens - 1):
+            total = total + near_in[j, part]
+        return total
+
     for side in range(2):
-        total = near[side]
-        for j in range(ens - 1):
-            total = total + near_in[j, side]
-        total = total * mass_in[side]
+        made = summed(side) * mass_in[side]
         for k, (n, dist) in enumerate(side_rows()):
-            row = HALO + cols + dist if side else HALO - 1 - n + dist
-            forcing[n, pl.ds(row, 1), :] = total[k:k + 1]
+            forcing[n, pl.ds(beyond[side](n, dist), 1), :] = made[k:k + 1]
+
+        @pl.when(far[side])
+        def _():
+            late_all.wait_recv()
+            made = summed(2) * mass[side]
+            for k, (n, dist) in enumerate(side_rows()):
+                forcing[n, pl.ds(own_edge[side](n, dist), 1), :] = made[k:k + 1]
     every = range(0, wide, 8)
-    inner = range(HALO, HALO + cols, 8)
     linear_step(forcing.at[pl.ds(2, 1)], state1, -1, consts, every, 0, wide, False, forcing.at[1])
     linear_step(state1, state2, -1, consts, every, 0, wide, True, forcing.at[0])
     linear_step(state2, state3, -1, consts, inner, 0, wide)
@@ -465,8 +484,12 @@
 
     each_peer(tell)
     load_v.wait()
-    for copy in f_copies + m_copies + n_copies + list(sums.values()):
+    for copy in f_copies:
         copy.wait_send()
+    all_of(arrived, SUM_COPY, 5).wait_send()
+    m_all.wait_send()
+    n_all.wait_send()
+    pl.when(is_end)(late_all.wait_send)
     everything = pltpu.make_async_remote_copy(
         src_ref=tiles, dst_ref=tiles, send_sem=tile_send, recv_sem=tile_recv,
         device_id=right_dev, device_id_type=MESH,
@@ -487,13 +510,14 @@
     control_new, residual_new, direction_new, sem,
 ):
     step_size, ratio = scalars[pl.ds(0, 1), pl.ds(0, 1)], scalars[pl.ds(1, 1), pl.ds(0, 1)]
-    ids = itertools.count()
-    copies = []
-
-    def send(src, dst, at):
-        copies.append(pltpu.make_async_copy(src.at[at], dst.at[at], sem.at[next(ids)]))
-        copies[-1].start()
-
+
+    def copy(which, src, dst, *at):
+        part = (src.at[at], dst.at[at]) if at else (src, dst)
+        return pltpu.make_async_copy(*part, sem.at[which])
+
+    pairs = (
+        (residual_new, residual_out), (direction_new, direction_out), (control_new, control_out)
+    )
     members, cols = control.shape[:2]
     for m in range(members):
         for h in range(2):
@@ -503,11 +527,10 @@
             residual_new[at] = new
             direction_new[at] = new + ratio * d
             control_new[at] = control[at] + step_size * d
-            send(residual_new, residual_out, at)
-            send(direction_new, direction_out, at)
-            send(control_new, control_out, at)
-    for copy in copies:
-        copy.wait()
+            for which, pair in enumerate(pairs):
+                copy(which, *pair, *at).start()
+    for which, pair in enumerate(pairs):
+        copy(which, *pair).wait()
 
 
 def body(ens, lon, control, residual, direction, ens_perturb, localize, obs_cell, obs_slot, obs_weight):
@@ -522,7 +545,6 @@
     dma = pltpu.SemaphoreType.DMA
     field = pltpu.VMEM((members, cols, lat), f32)
     vmem = pl.BlockSpec(memory_space=pltpu.VMEM)
-    copies = remote_count(ens, lat, nobs)
     outs = pl.pallas_call(
         functools.partial(kernel, ens, lon),
         out_shape=(field, field, field, field, pltpu.VMEM((8, 128), f32)),
@@ -548,13 +570,13 @@
             pltpu.VMEM((max(ens - 1, 1), 1, nobs), f32),
             pltpu.VMEM((STEPS * cols, lat), f32),
             pltpu.VMEM((STEPS, wide, lat), f32),
-            pltpu.VMEM((2, 8, lat), f32),
-            pltpu.VMEM((max(ens - 1, 1), 2, 8, lat), f32),
+            pltpu.VMEM((3, 8, lat), f32),
+            pltpu.VMEM((max(ens - 1, 1), 3, 8, lat), f32),
             pltpu.VMEM((2, 8, lat), f32),
             pltpu.VMEM((2, 8, lat), f32),
             pltpu.VMEM((count - 1, 1, 128), f32),
             pltpu.VMEM((1, 128), f32),
-            dma((8 + lat // BLOCK,)), dma((copies,)), dma((copies,)),
+            dma((10,)), dma((6,)), dma((4 + len(SHARES),)),
             dma, dma,
         ],
         compiler_params=pltpu.CompilerParams(
@@ -570,7 +592,7 @@
         out_shape=[jax.ShapeDtypeStruct((members, cols, lat), f32)] * 3,
         in_specs=[vmem] * 5,
         out_specs=[hbm] * 3,
-        scratch_shapes=[pltpu.VMEM((members, cols, lat), f32)] * 3 + [dma((6 * members,))],
+        scratch_shapes=[pltpu.VMEM((members, cols, lat), f32)] * 3 + [dma((3,))],
         compiler_params=pltpu.CompilerParams(vmem_limit_bytes=8 * 1024 * 1024),
     )(*outs)
     return tuple(map(flip, outs))

time: 28.3 us -> 27.5 us (0.972)
  Pallas kernels: 27.2 us -> 26.4 us
    pallas_call x1, Pallas kernels: 26 us -> 25.2 us  [body(): pl.pallas_call(functools.partial(kernel, ens, lon), out_shape=(field, fie...]
where the time goes in v4:
time: 27.5 us; the launch traced here: 27.2 us
  Pallas kernels  26.4 us (96%)
  between operations  0.8 us (3%)
    pallas_call x1, Pallas kernels, body(): pl.pallas_call(functools.partial(kernel, ens, lon), out_shape=(field, fie...  25.2 us
    pallas_call x1, Pallas kernels, body(): pl.pallas_call(update, out_shape=[jax.ShapeDtypeStruct((members, cols, la...  1.21 us

profile of v4, /device:TPU:0, one launch (start us, length us, event | category | flops | bytes accessed | tf_op | source)
XLA Modules:
  0.0 27.2 jit_solution(4491166746901696869)
XLA Ops:
  0.6 25.2 %shard_map.112 = (f32[2,64,1024]{2,1,0:T(8,128)S(1)}, f32[2,64,1024]{2,1,0:T(8,128)S(1)}, f32[2,64,1024]{2,1,0:T(8,128)S(1)}, f32[2,64,1024]{2,1,0:T(8,128)S(1)}, f32[8,128]{1,0:T(8,128)S(1)}) custom-call(f32[2,64,1024]{2,1,0:T(8,128)} %bitcast.11, f32[2,64,1024]{2,1,0:T(8,128)} %bitcast.12, f32[2,64,1024]{2,1,0:T(8,128)} %bitcast.13, ...), custom_call_target="tpu_custom_call" | custom-call | tf_op jit(solution)/shard_map/pallas_call | solution.py:548
  25.9 1.2 %shard_map.113 = (f32[2,64,1024]{2,1,0:T(8,128)}, f32[2,64,1024]{2,1,0:T(8,128)}, f32[2,64,1024]{2,1,0:T(8,128)}) custom-call(f32[2,64,1024]{2,1,0:T(8,128)S(1)} %get-tuple-element.11.control, f32[2,64,1024]{2,1,0:T(8,128)S(1)} %get-tuple-element.12.residual, f32[2,64,1024]{2,1,0:T(8,128)S(1)} %get-tuple-element.13.direction, ...), custom_call_target="tpu_custom_call" | custom-call | tf_op jit(solution)/shard_map/pallas_call | solution.py:590

commit v5 on v4

--- a/solution.py
+++ b/solution.py
@@ -36,47 +36,48 @@
 
 
 def linear_step(source, target, sign, consts, blocks, low_end, high_end, rest=True, extra=None):
-    lat = source.shape[2]
-    lon_c, cor_c = consts[0], consts[1]
+    panels = source.shape[2] // 128
+    row = lax.broadcasted_iota(jnp.int32, (8, 128), 0)
     lane = lax.broadcasted_iota(jnp.int32, (8, 128), 1)
 
     def less(value, term):
         return value - term if sign > 0 else value + term
 
-    for start in blocks:
-        here = pl.ds(start, 8)
-
-        def lon_diff(comp, block):
-            if start + 8 == high_end:
-                east = pltpu.roll(block, 7, 0)
+    for j in range(panels):
+        lanes = pl.ds(128 * j, 128)
+        lon_c, cor_c = consts[0, :, lanes], consts[1, :, lanes]
+
+        def tile(comp, start, panel):
+            return source[comp, pl.ds(start, 8), pl.ds(128 * panel, 128)]
+
+        def lon_diff(comp, start, block):
+            ahead = tile(comp, start + 8, j) if start + 8 < high_end else block
+            behind = tile(comp, start - 8, j) if start > low_end else block
+            east = pltpu.roll(jnp.where(row == 0, ahead, block), 7, 0)
+            west = pltpu.roll(jnp.where(row == 7, behind, block), 1, 0)
+            return lon_c * (east - west)
+
+        def lat_diff(comp, start, block):
+            ahead = tile(comp, start, j + 1) if j + 1 < panels else 0.0
+            behind = tile(comp, start, j - 1) if j else 0.0
+            up = pltpu.roll(jnp.where(lane == 0, ahead, block), 127, 1)
+            down = pltpu.roll(jnp.where(lane == 127, behind, block), 1, 1)
+            return HALF * (up - down)
+
+        for start in blocks:
+            here = pl.ds(start, 8)
+            height = tile(0, start, j)
+            along_lon, along_lat = lon_diff(0, start, height), lat_diff(0, start, height)
+            if rest:
+                zonal, merid = tile(1, start, j), tile(2, start, j)
+                new = less(height, lon_diff(1, start, zonal) + lat_diff(2, start, merid))
+                target[1, here, lanes] = less(zonal, along_lon - cor_c * merid)
+                target[2, here, lanes] = less(merid, along_lat + cor_c * zonal)
             else:
-                east = source[comp, pl.ds(start + 1, 8), :]
-            if start == low_end:
-                west = pltpu.roll(block, 1, 0)
-            else:
-                west = source[comp, pl.ds(start - 1, 8), :]
-            return lon_c * (east - west)
-
-        def lat_diff(block):
-            up, down = pltpu.roll(block, lat - 1, 1), pltpu.roll(block, 1, 1)
-            up_end = jnp.where(lane == 127, 0.0, up[:, lat - 128:])
-            down_end = jnp.where(lane == 0, 0.0, down[:, :128])
-            up = jnp.concatenate([up[:, :lat - 128], up_end], axis=1)
-            down = jnp.concatenate([down_end, down[:, 128:]], axis=1)
-            return HALF * (up - down)
-
-        height = source[0, here, :]
-        along_lon, along_lat = lon_diff(0, height), lat_diff(height)
-        if rest:
-            zonal, merid = source[1, here, :], source[2, here, :]
-            new = less(height, lon_diff(1, zonal) + lat_diff(merid))
-            target[1, here, :] = less(zonal, along_lon - cor_c * merid)
-            target[2, here, :] = less(merid, along_lat + cor_c * zonal)
-        else:
-            new = height
-            target[1, here, :] = less(0.0, along_lon)
-            target[2, here, :] = less(0.0, along_lat)
-        target[0, here, :] = new if extra is None else new + extra[here, :]
+                new = height
+                target[1, here, lanes] = less(0.0, along_lon)
+                target[2, here, lanes] = less(0.0, along_lat)
+            target[0, here, lanes] = new if extra is None else new + extra[here, lanes]
 
 
 def fold(values):

time: 27.5 us -> 27.1 us (0.985)
  Pallas kernels: 26.4 us -> 26 us
    pallas_call x1, Pallas kernels: 25.2 us -> 24.8 us  [body(): pl.pallas_call(functools.partial(kernel, ens, lon), out_shape=(field, fie...]
where the time goes in v5:
time: 27.1 us; the launch traced here: 26.8 us
  Pallas kernels  26 us (96%)
  between operations  0.8 us (3%)
    pallas_call x1, Pallas kernels, body(): pl.pallas_call(functools.partial(kernel, ens, lon), out_shape=(field, fie...  24.8 us
    pallas_call x1, Pallas kernels, body(): pl.pallas_call(update, out_shape=[jax.ShapeDtypeStruct((members, cols, la...  1.21 us

profile of v5, /device:TPU:0, one launch (start us, length us, event | category | flops | bytes accessed | tf_op | source)
XLA Modules:
  0.0 26.8 jit_solution(3025472614489273860)
XLA Ops:
  0.6 24.8 %shard_map.112 = (f32[2,64,1024]{2,1,0:T(8,128)S(1)}, f32[2,64,1024]{2,1,0:T(8,128)S(1)}, f32[2,64,1024]{2,1,0:T(8,128)S(1)}, f32[2,64,1024]{2,1,0:T(8,128)S(1)}, f32[8,128]{1,0:T(8,128)S(1)}) custom-call(f32[2,64,1024]{2,1,0:T(8,128)} %bitcast.11, f32[2,64,1024]{2,1,0:T(8,128)} %bitcast.12, f32[2,64,1024]{2,1,0:T(8,128)} %bitcast.13, ...), custom_call_target="tpu_custom_call" | custom-call | tf_op jit(solution)/shard_map/pallas_call | solution.py:549
  25.5 1.2 %shard_map.113 = (f32[2,64,1024]{2,1,0:T(8,128)}, f32[2,64,1024]{2,1,0:T(8,128)}, f32[2,64,1024]{2,1,0:T(8,128)}) custom-call(f32[2,64,1024]{2,1,0:T(8,128)S(1)} %get-tuple-element.11.control, f32[2,64,1024]{2,1,0:T(8,128)S(1)} %get-tuple-element.12.residual, f32[2,64,1024]{2,1,0:T(8,128)S(1)} %get-tuple-element.13.direction, ...), custom_call_target="tpu_custom_call" | custom-call | tf_op jit(solution)/shard_map/pallas_call | solution.py:591
